TPU v7x, 128 devices: a whole 4x4x4 slice. The times are simulated.
128 devices in a mesh: row: 16 (over z_hi, y, core), col: 8 (over x, z_lo).
Axes of the slice: x: 4, y: 4, z: 4 (z_hi: 2, z_lo: 2; z = z_hi * 2 + z_lo), core: 2. Of those that a mesh axis runs over, the one named last changes fastest.
Arguments:
- alignment_tensor: bfloat16 [128, 1024, 256], P(None, ('row', 'col')), may hold values from -6 to 6
- alignment_scaling_vector: float32 [256], replicated, may hold values from 0.1 to 1.9
- first_factor_matrix: bfloat16 [256, 32], replicated, may hold values from -0.375 to 0.375
- second_factor_matrix: bfloat16 [256, 32], replicated, may hold values from -0.375 to 0.375
- final_mapping_matrix: bfloat16 [1024, 128], replicated, may hold values from -2 to 2
- final_offset_vector: float32 [128], replicated, may hold values from -3 to 3
- couple_tensor: bfloat16 [1024, 1024, 128], P('row', 'col'), may hold values from -6 to 6
- feedforward_scaling_vector: float32 [128], replicated, may hold values from 0.1 to 1.9
- feedforward_expand_matrix: bfloat16 [128, 512], replicated, may hold values from -0.5 to 0.5
- feedforward_contract_matrix: bfloat16 [512, 128], replicated, may hold values from -0.25 to 0.25
- upstream_sensitivity: bfloat16 [1024, 1024, 128], P('row', 'col'), may hold values from -6 to 6
Outputs:
- couple_revised_tensor: bfloat16 [1024, 1024, 128], P('row', 'col')
- couple_sensitivity: bfloat16 [1024, 1024, 128], P('row', 'col')
- alignment_sensitivity: bfloat16 [128, 1024, 256], P(None, ('row', 'col'))
- grad_out_proj: float32 [1024, 128], replicated
- grad_trans_in: float32 [128, 512], replicated
- grad_trans_out: float32 [512, 128], replicated
- first_factor_matrix_sensitivity: float32 [256, 32], replicated
- second_factor_matrix_sensitivity: float32 [256, 32], replicated
All inputs are finite; a program needn't handle non-finite values.
Results may differ from a plain program's by a relative error of at most 0.02.
Values may be sent and summed in bfloat16 or wider, within the bound.
No kernel may reach another device: no remote copies, remote signals or barrier semaphores. Data moves between devices by JAX's collectives and lax.ppermute only.
A program may use at most 64 MiB of HBM per device.

v0:
```python
import jax
import jax.numpy as jnp
from jax import lax
from jax.sharding import PartitionSpec as P

EPSILON = 1e-05
ROOT_HALF = 0.7071067811865476
INV_ROOT_TWO_PI = 0.3989422804014327


def sent_together(arrays, axis, dim, along):
    widths = [a.shape[along] for a in arrays]
    both = jnp.concatenate(arrays, axis=along)
    out = lax.all_gather(both, axis, axis=dim, tiled=True)
    return tuple(jnp.split(out, [sum(widths[:k]) for k in range(1, len(widths))], axis=along))


def broadcast(x, axis, root):
    return lax.dynamic_index_in_dim(lax.all_gather(x, axis), root, 0, keepdims=False)


def in_blocks(x, dim, count):
    before, after = (x.shape[:dim], x.shape[dim + 1 :])
    return jnp.moveaxis(x.reshape(*before, count, -1, *after), dim, 0)


def sent_and_summed(x, axis, dim):
    count = lax.axis_size(axis)
    parts = lax.all_to_all(in_blocks(x, dim, count), axis, 0, 0, tiled=True)
    return jnp.sum(parts.astype(jnp.float32), axis=0)


def in_one(arrays, axis):
    ravelled, at, outs = (jnp.concatenate([a.reshape(-1) for a in arrays]), 0, [])
    so_far = lax.psum(ravelled, axis)
    for a in arrays:
        outs.append(so_far[at : at + a.size].reshape(a.shape))
        at += a.size
    return tuple(outs)


def smooth_gate(values):
    return 0.5 * values * (1.0 + jax.scipy.special.erf(values * ROOT_HALF))


def smooth_slope(values):
    return (
        0.5 * (1.0 + jax.scipy.special.erf(values * ROOT_HALF))
        + values * jnp.exp(-0.5 * values * values) * INV_ROOT_TWO_PI
    )


def standardize_features(values, gain_vec):
    average = jnp.mean(values, axis=-1, keepdims=True)
    centred = values - average
    variance = jnp.mean(centred * centred, axis=-1, keepdims=True)
    inv_scale = lax.rsqrt(variance + EPSILON)
    vhat_values = centred * inv_scale
    return (vhat_values * gain_vec, vhat_values, inv_scale)


def standardize_reverse_mode(incoming, vhat_values, inv_scale, gain_vec):
    scaled = incoming * gain_vec
    return inv_scale * (
        scaled
        - jnp.mean(scaled, axis=-1, keepdims=True)
        - vhat_values * jnp.mean(scaled * vhat_values, axis=-1, keepdims=True)
    )


def on_device(
    alignment_tensor,
    alignment_scaling_vector,
    first_factor_matrix,
    second_factor_matrix,
    final_mapping_matrix,
    final_offset_vector,
    couple_tensor,
    feedforward_scaling_vector,
    feedforward_expand_matrix,
    feedforward_contract_matrix,
    upstream_sensitivity,
):
    aligned_number, shard_extent, alignment_feature_size = alignment_tensor.shape
    channels = first_factor_matrix.shape[1]
    row_count, col_count, pair_width = couple_tensor.shape
    amino_number = row_count * lax.axis_size("row")
    col_at = lax.axis_index("col")
    rescaled_complete_lines, alignment_centered_scaled, alignment_reciprocal_spread = (
        standardize_features(alignment_tensor.astype(jnp.float32), alignment_scaling_vector)
    )
    rescaled_lines = rescaled_complete_lines.astype(jnp.bfloat16)
    left_local = jnp.einsum(
        "srm,mc->rcs", rescaled_lines, first_factor_matrix, preferred_element_type=jnp.float32
    ).astype(jnp.bfloat16)
    right_local = jnp.einsum(
        "srm,mc->rcs", rescaled_lines, second_factor_matrix, preferred_element_type=jnp.float32
    ).astype(jnp.bfloat16)
    row_ratio = lax.axis_size("row") // lax.axis_size("col")
    left_rows, right_rows = sent_together((left_local, right_local), "col", 0, 1)
    pieces = []
    for member in range(row_ratio):
        pieces.append(broadcast(right_rows, "row", col_at * row_ratio + member))
    right_cols = jnp.concatenate(pieces, axis=0)
    block_rows = 8

    def block_step(totals, start_row):
        acc_right, summed_result_state, summed_entry_state, summed_feedforward_result = totals
        left_block = lax.dynamic_slice_in_dim(left_rows, start_row, block_rows, 0)
        outer_prod = (
            jnp.einsum("ics,jes->ijce", left_block, right_cols, preferred_element_type=jnp.float32)
            / aligned_number
        ).astype(jnp.bfloat16)
        outer_prod = outer_prod.reshape(block_rows * col_count, channels * channels)
        pair_block = lax.dynamic_slice_in_dim(couple_tensor, start_row, block_rows, 0).reshape(
            -1, pair_width
        )
        cot_block = lax.dynamic_slice_in_dim(
            upstream_sensitivity, start_row, block_rows, 0
        ).reshape(-1, pair_width)
        update = (
            jnp.dot(outer_prod, final_mapping_matrix, preferred_element_type=jnp.float32)
            + final_offset_vector
        )
        middle = (pair_block.astype(jnp.float32) + update).astype(jnp.bfloat16)
        middle_full = middle.astype(jnp.float32)
        normed_pair_full, pair_hat, pair_inv = standardize_features(
            middle_full, feedforward_scaling_vector
        )
        normed_pair = normed_pair_full.astype(jnp.bfloat16)
        pre_gate = jnp.dot(
            normed_pair, feedforward_expand_matrix, preferred_element_type=jnp.float32
        )
        hidden = smooth_gate(pre_gate).astype(jnp.bfloat16)
        result = (
            middle_full
            + jnp.dot(hidden, feedforward_contract_matrix, preferred_element_type=jnp.float32)
        ).astype(jnp.bfloat16)
        summed_feedforward_result = summed_feedforward_result + jnp.einsum(
            "pk,pn->kn", hidden, cot_block, preferred_element_type=jnp.float32
        )
        hidden_grad = (
            jnp.dot(cot_block, feedforward_contract_matrix.T, preferred_element_type=jnp.float32)
            * smooth_slope(pre_gate)
        ).astype(jnp.bfloat16)
        summed_entry_state = summed_entry_state + jnp.einsum(
            "pk,pn->kn", normed_pair, hidden_grad, preferred_element_type=jnp.float32
        )
        norm_grad = jnp.dot(
            hidden_grad, feedforward_expand_matrix.T, preferred_element_type=jnp.float32
        )
        grad_block = (
            cot_block.astype(jnp.float32)
            + standardize_reverse_mode(norm_grad, pair_hat, pair_inv, feedforward_scaling_vector)
        ).astype(jnp.bfloat16)
        summed_result_state = summed_result_state + jnp.einsum(
            "pk,pn->kn", outer_prod, grad_block, preferred_element_type=jnp.float32
        )
        outer_grad = jnp.dot(
            grad_block, final_mapping_matrix.T, preferred_element_type=jnp.float32
        ).astype(jnp.bfloat16)
        outer_grad = outer_grad.reshape(block_rows, col_count, channels, channels)
        left_part = (
            jnp.einsum("ijce,jes->ics", outer_grad, right_cols, preferred_element_type=jnp.float32)
            / aligned_number
        )
        acc_right = (
            acc_right
            + jnp.einsum(
                "ijce,ics->jes", outer_grad, left_block, preferred_element_type=jnp.float32
            )
            / aligned_number
        )
        return (
            (acc_right, summed_result_state, summed_entry_state, summed_feedforward_result),
            (result, grad_block, left_part),
        )

    initial = (
        jnp.zeros((col_count, channels, aligned_number), jnp.float32),
        jnp.zeros((channels * channels, pair_width), jnp.float32),
        jnp.zeros(feedforward_expand_matrix.shape, jnp.float32),
        jnp.zeros(feedforward_contract_matrix.shape, jnp.float32),
    )
    starts = jnp.arange(row_count // block_rows, dtype=jnp.int32) * block_rows
    totals, stacked = lax.scan(block_step, initial, starts)
    acc_right, summed_result_state, summed_entry_state, summed_feedforward_result = totals
    results, grad_blocks, left_parts = stacked
    couple_revised_tensor = results.reshape(row_count, col_count, pair_width)
    couple_sensitivity = grad_blocks.reshape(row_count, col_count, pair_width)
    left_parts = left_parts.reshape(row_count, channels, aligned_number)
    left_grad = sent_and_summed(left_parts.astype(jnp.bfloat16), "col", 0).astype(jnp.bfloat16)
    col_total = lax.axis_size("col")
    grouped = acc_right.reshape(row_ratio, col_total, shard_extent * channels, aligned_number)
    routed = lax.all_to_all(
        grouped.astype(jnp.bfloat16), "col", split_axis=1, concat_axis=0, tiled=True
    ).astype(grouped.dtype)
    routed = routed.reshape(row_ratio * col_total * shard_extent, channels, aligned_number)
    right_grad = sent_and_summed(routed.astype(jnp.bfloat16), "row", 0).astype(jnp.bfloat16)
    left_weight = jnp.einsum(
        "srm,rcs->mc", rescaled_lines, left_grad, preferred_element_type=jnp.float32
    )
    right_weight = jnp.einsum(
        "srm,rcs->mc", rescaled_lines, right_grad, preferred_element_type=jnp.float32
    )
    rescaled_sensitivity = jnp.einsum(
        "rcs,mc->srm", left_grad, first_factor_matrix, preferred_element_type=jnp.float32
    )
    rescaled_sensitivity = rescaled_sensitivity + jnp.einsum(
        "rcs,mc->srm", right_grad, second_factor_matrix, preferred_element_type=jnp.float32
    )
    alignment_sensitivity = standardize_reverse_mode(
        rescaled_sensitivity,
        alignment_centered_scaled,
        alignment_reciprocal_spread,
        alignment_scaling_vector,
    ).astype(jnp.bfloat16)
    summed = in_one(
        (
            summed_result_state,
            summed_entry_state,
            summed_feedforward_result,
            left_weight,
            right_weight,
        ),
        ("row", "col"),
    )
    return (
        couple_revised_tensor,
        couple_sensitivity,
        alignment_sensitivity,
        summed[0] / amino_number,
        summed[1] / amino_number,
        summed[2] / amino_number,
        summed[3] / amino_number,
        summed[4] / amino_number,
    )


def solution(mesh):
    return jax.shard_map(
        on_device,
        mesh=mesh,
        in_specs=(
            P(None, ("row", "col"), None),
            P(),
            P(),
            P(),
            P(),
            P(),
            P("row", "col", None),
            P(),
            P(),
            P(),
            P("row", "col", None),
        ),
        out_specs=(
            P("row", "col", None),
            P("row", "col", None),
            P(None, ("row", "col"), None),
            P(),
            P(),
            P(),
            P(),
            P(),
        ),
        check_vma=False,
    )
```

profile of v0, /device:TPU:1, one launch (start us, length us, event | category | flops | bytes accessed | tf_op | source)
XLA Modules:
  0.0 594.1 jit_solution(380368857876688785)
XLA Ops:
  12.8 36.9 %all-gather.4.cloned.1.call-done = bf16[64,64,128]{2,1,0:T(8,128)(2,1)} async-done(((bf16[8,64,128]{2,1,0:T(8,128)(2,1)}), bf16[64,64,128]{2,1,0:T(8,128)(2,1)}) %all-gather.4.cloned.1.call-update) | async-done | bytes 1048592 | tf_op jit(solution)/shard_map/all_gather | solution.py:14
  51.9 78.5 %all-gather.6.cloned.1.call-done = bf16[1024,32,128]{2,1,0:T(8,128)(2,1)} async-done(((bf16[64,32,128]{2,1,0:T(8,128)(2,1)}), bf16[1024,32,128]{2,1,0:T(8,128)(2,1)}) %all-gather.6.cloned.1.call-update) | async-done | bytes 8388624 | tf_op jit(solution)/shard_map/all_gather | solution.py:19
  132.7 246.7 %while.23 = (s32[]{:T(128)}, f32[128,32,128]{2,0,1:T(8,128)}, f32[1024,128]{1,0:T(8,128)}, f32[128,512]{1,0:T(8,128)S(1)}, f32[512,128]{1,0:T(8,128)S(1)}, /*ind...) while((s32[]{:T(128)}, f32[128,32,128]{2,0,1:T(8,128)}, ...), condition=%wide.region_7.8_spmd.clone, body=%wide.region_2.7_spmd.clone.sunk | while | flops 2433516544 | bytes 108827968 | solution.py:186
  154.1 2.6 copy.166
  156.7 2.2 copy.167
  185.0 2.6 copy.166
  187.5 2.2 copy.167
  215.8 2.6 copy.166
  218.4 2.2 copy.167
  246.6 2.6 copy.166
  249.2 2.2 copy.167
  277.5 2.6 copy.166
  280.1 2.2 copy.167
  308.3 2.6 copy.166
  339.2 2.6 copy.166
  370.0 2.6 copy.166
  379.4 4.1 all-to-all-start
  383.5 2.8 copy.147
  387.4 5.3 all-to-all-done
  392.7 4.2 all-to-all-start.1
  398.6 13.3 %all-to-all-done.1 = bf16[2,8,256,128]{3,2,0,1:T(8,128)(2,1)} async-done(((bf16[2,8,256,128]{3,2,0,1:T(8,128)(2,1)}), bf16[2,8,256,128]{3,2,0,1:T(8,128)(2,1)}, u32[]{:S(2)}, u32[]{:S(2)}) %all-to-all-start.1) | async-done | bytes 1048608 | tf_op jit(solution)/shard_map/all_to_all | solution.py:195
  411.8 5.9 all-to-all-start.2
  420.3 14.6 %all-to-all-done.2 = bf16[16,8,32,128]{3,2,1,0:T(8,128)(2,1)S(1)} async-done(((bf16[16,8,32,128]{3,2,1,0:T(8,128)(2,1)}), bf16[16,8,32,128]{3,2,1,0:T(8,128)(2,1)S(1)}, u32[]{:S(2)}, u32[]{:S(2)}) %all-to-all-start.2) | async-done | bytes 1048608 | tf_op jit(solution)/shard_map/all_to_all | solution.py:29
  439.3 141.5 %all-reduce.2.cloned.1.call-done = f32[278528]{0:T(1024)} async-done(((f32[278528]{0:T(1024)}), f32[278528]{0:T(1024)}) %all-reduce.2.cloned.1.call-update) | async-done | bytes 1114128 | tf_op jit(solution)/shard_map/psum | solution.py:35
  (747 shorter events, 222.2 us)
Async XLA Ops:
  7.2 4.4 copy-start.11
  7.2 4.4 copy-start.36
  7.2 4.4 copy-start.34
  7.2 42.5 %all-gather.4.cloned.1.call-start = ((), (), s32[]{:S(2)}) async-start(), calls=%async_computation.3 | async-start | bytes 1179648 | tf_op jit(solution)/shard_map/all_gather | solution.py:14
  8.6 3.5 copy-start.30
  12.8 117.6 %all-gather.6.cloned.1.call-start = ((), (), s32[]{:S(2)}) async-start(), calls=%async_computation.5 | async-start | bytes 8912896 | tf_op jit(solution)/shard_map/all_gather | solution.py:19
  132.7 4.4 copy-start.18
  163.6 4.5 copy-start.18
  194.4 4.5 copy-start.18
  225.2 4.5 copy-start.18
  256.1 4.5 copy-start.18
  286.9 4.5 copy-start.18
  317.8 4.5 copy-start.18
  348.6 4.5 copy-start.18
  379.4 13.2 %all-to-all-start = ((bf16[8,8,32,128]{3,1,2,0:T(8,128)(2,1)}), bf16[8,8,32,128]{3,1,2,0:T(8,128)(2,1)S(1)}, u32[]{:S(2)}, u32[]{:S(2)}) async-start(bf16[8,8,32,128]{3,1,2,0:T(8,128)(2,1)} %get-tuple-element.532), calls=%async_computation | async-start | bytes 1048576 | tf_op jit(solution)/shard_map/all_to_all | solution.py:29
  386.3 10.6 %copy-start.27 = (f32[1024,128]{1,0:T(8,128)S(1)}, f32[1024,128]{1,0:T(8,128)}, u32[]{:S(2)}) copy-start(f32[1024,128]{1,0:T(8,128)} %get-tuple-element.527) | copy-start | bytes 1572868
  392.7 19.1 %all-to-all-start.1 = ((bf16[2,8,256,128]{3,2,0,1:T(8,128)(2,1)}), bf16[2,8,256,128]{3,2,0,1:T(8,128)(2,1)}, u32[]{:S(2)}, u32[]{:S(2)}) async-start(bf16[2,8,256,128]{3,2,0,1:T(8,128)(2,1)} %copy.80), calls=%async_computation.1 | async-start | bytes 2097152 | tf_op jit(solution)/shard_map/all_to_all | solution.py:195
  397.8 20.8 %copy-start.12 = (bf16[128,8,256]{2,1,0:T(8,128)(2,1)S(1)}, bf16[128,8,256]{2,1,0:T(8,128)(2,1)}, u32[]{:S(2)}) copy-start(bf16[128,8,256]{2,1,0:T(8,128)(2,1)} %param.13) | copy-start | bytes 1572868
  397.8 20.8 %copy-start.31 = (f32[128,8]{0,1:T(8,128)S(1)}, f32[128,8]{0,1:T(8,128)}, u32[]{:S(2)}) copy-start(f32[128,8]{0,1:T(8,128)} %copy-done.30) | copy-start | bytes 12292
  397.8 20.8 %copy-start.33 = (f32[128,8]{0,1:T(8,128)S(1)}, f32[128,8]{0,1:T(8,128)}, u32[]{:S(2)}) copy-start(f32[128,8]{0,1:T(8,128)} %copy-done.32) | copy-start | bytes 12292
  397.8 20.8 %copy-start.37 = (f32[256]{0:T(256)S(1)}, f32[256]{0:T(256)}, u32[]{:S(2)}) copy-start(f32[256]{0:T(256)} %param.14) | copy-start | bytes 3076
  411.8 8.2 %copy-start.35 = (bf16[256,32]{0,1:T(8,128)(2,1)S(1)}, bf16[256,32]{0,1:T(8,128)(2,1)}, u32[]{:S(2)}) copy-start(bf16[256,32]{0,1:T(8,128)(2,1)} %param.15) | copy-start | bytes 49156
  411.8 23.1 %all-to-all-start.2 = ((bf16[16,8,32,128]{3,2,1,0:T(8,128)(2,1)}), bf16[16,8,32,128]{3,2,1,0:T(8,128)(2,1)S(1)}, u32[]{:S(2)}, u32[]{:S(2)}) async-start(bf16[16,8,32,128]{3,2,1,0:T(8,128)(2,1)} %bitcast.12), calls=%async_computation.2 | async-start | bytes 2097152 | tf_op jit(solution)/shard_map/all_to_all | solution.py:29
  417.7 163.1 %all-reduce.2.cloned.1.call-start = ((), (), s32[]{:S(2)}) async-start(), calls=%async_computation.4 | async-start | bytes 2228224 | tf_op jit(solution)/shard_map/psum | solution.py:35
  (212 other events, 367.7 us)
Sparse Core Ops, SparseCore 0:
  12.9 36.7 all-gather.3
  52.2 78.2 all-gather.5
  437.6 143.1 all-reduce.1
where the time goes:
time: 597 us; the launch traced here: 594 us
  waiting for transfers between devices  290 us (49%)
  local copies, waits for them, and re-layouts  147 us (25%)
  matrix products  98.2 us (16%)
  loops' own time  19 us (3%)
  starting transfers between devices  14.3 us (2%)
  between operations  14.2 us (2%)
  other arithmetic  11.1 us (2%)
    psum x1, waiting for transfers between devices, in_one(): so_far = lax.psum(ravelled, axis)  141 us
    all_gather x1, waiting for transfers between devices, broadcast(): lax.all_gather(x, axis)  78.5 us
    while x440, local copies, waits for them, and re-layouts  45.3 us
    all_gather x1, waiting for transfers between devices, sent_together(): out = lax.all_gather(both, axis, axis=dim, tiled=True)  36.9 us
    dynamic_update_slice x24, local copies, waits for them, and re-layouts, on_device(): totals, stacked = lax.scan(block_step, initial, starts)  20.9 us
    convert_element_type x8, local copies, waits for them, and re-layouts, block_step(): outer_grad = jnp.dot(grad_block, final_mapping_matrix.T, preferred_elemen...  20.6 us
    all_to_all x2, waiting for transfers between devices, sent_and_summed(): parts = lax.all_to_all(in_blocks(x, dim, count), axis, 0, 0, tiled=True)  19.9 us
    another operation x1, loops' own time, on_device(): totals, stacked = lax.scan(block_step, initial, starts)  19 us
  transfers between devices with their start and end apart: 6, of which 6 were waited for; matrix products, arithmetic and copies ran while one was open for 2% of the time, Pallas kernels for 0%

commit v1 on v0

v1 whole, which is shorter than its diff:
```python
import jax
import jax.numpy as jnp
from jax import lax
from jax.experimental import pallas as pl
from jax.experimental.pallas import tpu as pltpu
from jax.sharding import PartitionSpec as P

EPSILON = 1e-05
ROOT_HALF = 0.7071067811865476
INV_ROOT_TWO_PI = 0.3989422804014327

F32 = jnp.float32
BF16 = jnp.bfloat16
BOTH = ("row", "col")


def matmul(a, b):
    return lax.dot_general(a, b, (((1,), (0,)), ((), ())), preferred_element_type=F32)


def matmul_nt(a, b):
    return lax.dot_general(a, b, (((1,), (1,)), ((), ())), preferred_element_type=F32)


def standardize_features(values, gain_vec):
    average = jnp.mean(values, axis=-1, keepdims=True)
    centred = values - average
    variance = jnp.mean(centred * centred, axis=-1, keepdims=True)
    inv_scale = lax.rsqrt(variance + EPSILON)
    vhat_values = centred * inv_scale
    return (vhat_values * gain_vec, vhat_values, inv_scale)


def standardize_reverse_mode(incoming, vhat_values, inv_scale, gain_vec):
    scaled = incoming * gain_vec
    return inv_scale * (
        scaled
        - jnp.mean(scaled, axis=-1, keepdims=True)
        - vhat_values * jnp.mean(scaled * vhat_values, axis=-1, keepdims=True)
    )


def pair_kernel(
    left_ref,
    right_t_ref,
    pair_ref,
    cot_ref,
    proj_ref,
    proj_t_ref,
    expand_ref,
    expand_t_ref,
    contract_ref,
    contract_t_ref,
    offset_ref,
    gain_ref,
    result_ref,
    grad_ref,
    d_left_ref,
    d_right_ref,
    g_proj_ref,
    g_expand_ref,
    g_contract_ref,
    right_scr,
    outer_scr,
    d_outer_scr,
    acc_right,
):
    step = pl.program_id(0)
    rows, seqs = left_ref.shape
    wide = right_t_ref.shape[0]
    width = proj_t_ref.shape[0]
    lanes = pair_ref.shape[1]
    channels = wide // lanes
    block = pair_ref.shape[0]

    @pl.when(step == 0)
    def _():
        for e in range(channels):
            at = slice(e * lanes, (e + 1) * lanes)
            right_scr[:, at] = right_t_ref[at, :].T
        acc_right[...] = jnp.zeros_like(acc_right)
        g_proj_ref[...] = jnp.zeros_like(g_proj_ref)
        g_expand_ref[...] = jnp.zeros_like(g_expand_ref)
        g_contract_ref[...] = jnp.zeros_like(g_contract_ref)

    left = left_ref[...]
    chunk = 2 * lanes
    for t in range(wide // chunk):
        at = slice(t * chunk, (t + 1) * chunk)
        outer_scr[:, at] = matmul(left, right_scr[:, at]).astype(BF16)

    gain = gain_ref[...]
    offset = offset_ref[...]

    def columns(scr, i):
        start = pl.multiple_of(i * channels, channels)
        tiles = [
            scr[pl.ds(start, channels), e * lanes : (e + 1) * lanes] for e in range(channels)
        ]
        return jnp.concatenate(tiles, axis=0)

    def beside(ref, i):
        return jnp.concatenate([ref[i].T, ref[i + 1].T], axis=1)

    def two_rows(p, carry):
        i = 2 * p
        outer = jnp.concatenate([columns(outer_scr, i), columns(outer_scr, i + 1)], axis=1)
        update = matmul(proj_t_ref[...], outer) + offset
        middle = (beside(pair_ref, i).astype(F32) + update).astype(BF16).astype(F32)
        average = jnp.sum(middle, axis=0, keepdims=True) * (1.0 / width)
        centred = middle - average
        variance = jnp.sum(centred * centred, axis=0, keepdims=True) * (1.0 / width)
        inv = lax.rsqrt(variance + EPSILON)
        vhat = centred * inv
        normed = (vhat * gain).astype(BF16)
        pre = matmul(expand_t_ref[...], normed)
        half = 0.5 * (1.0 + lax.erf(pre * ROOT_HALF))
        hidden = (pre * half).astype(BF16)
        slope = half + pre * jnp.exp(-0.5 * pre * pre) * INV_ROOT_TWO_PI
        result = (middle + matmul(contract_t_ref[...], hidden)).astype(BF16)
        result_ref[i] = result[:, :lanes].T
        result_ref[i + 1] = result[:, lanes:].T
        cot = beside(cot_ref, i)
        d_hidden = (matmul(contract_ref[...], cot) * slope).astype(BF16)
        g_contract_ref[...] += matmul_nt(hidden, cot)
        g_expand_ref[...] += matmul_nt(d_hidden, normed)
        q = matmul(expand_ref[...], d_hidden) * gain
        q_mean = jnp.sum(q, axis=0, keepdims=True) * (1.0 / width)
        q_hat = jnp.sum(q * vhat, axis=0, keepdims=True) * (1.0 / width)
        grad = (cot.astype(F32) + inv * (q - q_mean - vhat * q_hat)).astype(BF16)
        grad_ref[i] = grad[:, :lanes].T
        grad_ref[i + 1] = grad[:, lanes:].T
        g_proj_ref[...] += matmul_nt(outer, grad)
        d_outer = matmul(proj_ref[...], grad).astype(BF16)
        for k in range(2):
            start = pl.multiple_of((i + k) * channels, channels)
            for e in range(channels):
                d_outer_scr[pl.ds(start, channels), e * lanes : (e + 1) * lanes] = d_outer[
                    e * channels : (e + 1) * channels, k * lanes : (k + 1) * lanes
                ]
        return carry

    lax.fori_loop(0, block // 2, two_rows, 0)

    d_left_ref[...] = (matmul(d_outer_scr[...], right_t_ref[...]) * (1.0 / seqs)).astype(BF16)
    left_t = left.T
    for t in range(wide // chunk):
        at = slice(t * chunk, (t + 1) * chunk)
        acc_right[:, at] += matmul(left_t, d_outer_scr[:, at])

    @pl.when(step == pl.num_programs(0) - 1)
    def _():
        parts = d_right_ref.shape[0]
        each = d_right_ref.shape[2]
        for e in range(channels):
            tile = acc_right[:, e * lanes : (e + 1) * lanes].T
            d_right_ref[:, e] = tile.reshape(parts, each, seqs).astype(BF16)


def pair_stage(left, right_t, pair, cot, proj, expand, contract, offset, gain, each):
    rows, lanes, width = pair.shape
    seqs = left.shape[1]
    wide = right_t.shape[0]
    channels = wide // lanes
    hidden = expand.shape[1]
    block = 8
    by_e = (
        proj.reshape(channels, channels, width).transpose(1, 0, 2).reshape(channels * channels, width)
    )
    column = lambda v: jnp.broadcast_to(v.astype(F32)[:, None], (width, 2 * lanes))
    whole = lambda shape: pl.BlockSpec(shape, lambda b: (0,) * len(shape))
    tiles = pl.BlockSpec((block, lanes, width), lambda b: (b, 0, 0))
    flat = pl.BlockSpec((block * channels, seqs), lambda b: (b, 0))
    out = pl.pallas_call(
        pair_kernel,
        grid=(rows // block,),
        in_specs=[
            flat,
            whole((wide, seqs)),
            tiles,
            tiles,
            whole((channels * channels, width)),
            whole((width, channels * channels)),
            whole((width, hidden)),
            whole((hidden, width)),
            whole((hidden, width)),
            whole((width, hidden)),
            whole((width, 2 * lanes)),
            whole((width, 2 * lanes)),
        ],
        out_specs=[
            tiles,
            tiles,
            flat,
            whole((lanes // each, channels, each, seqs)),
            whole((channels * channels, width)),
            whole((hidden, width)),
            whole((hidden, width)),
        ],
        out_shape=[
            jax.ShapeDtypeStruct((rows, lanes, width), BF16),
            jax.ShapeDtypeStruct((rows, lanes, width), BF16),
            jax.ShapeDtypeStruct((rows * channels, seqs), BF16),
            jax.ShapeDtypeStruct((lanes // each, channels, each, seqs), BF16),
            jax.ShapeDtypeStruct((channels * channels, width), F32),
            jax.ShapeDtypeStruct((hidden, width), F32),
            jax.ShapeDtypeStruct((hidden, width), F32),
        ],
        scratch_shapes=[
            pltpu.VMEM((seqs, wide), BF16),
            pltpu.VMEM((block * channels, wide), BF16),
            pltpu.VMEM((block * channels, wide), BF16),
            pltpu.VMEM((seqs, wide), F32),
        ],
        compiler_params=pltpu.CompilerParams(
            dimension_semantics=("arbitrary",), vmem_limit_bytes=56 * 1024 * 1024
        ),
        name="pair_stage",
    )(
        left,
        right_t,
        pair,
        cot,
        by_e,
        by_e.T,
        expand,
        expand.T,
        contract,
        contract.T,
        column(offset),
        column(gain),
    )
    result, grad, d_left, d_right, g_proj, g_expand, g_contract = out
    return result, grad, d_left, d_right, g_proj, g_expand, g_contract


def spread(x, axis):
    count = lax.axis_size(axis)
    return lax.all_to_all(
        jnp.broadcast_to(x[None], (count, *x.shape)), axis, 0, 0, tiled=True
    )


def exchange(x, axis):
    return lax.all_to_all(x, axis, 0, 0, tiled=True)


def swap_pairs(rows, cols):
    ratio = rows // cols
    return [
        (r * cols + c, (c * ratio + r % ratio) * cols + r // ratio)
        for r in range(rows)
        for c in range(cols)
    ]


def on_device(
    alignment_tensor,
    alignment_scaling_vector,
    first_factor_matrix,
    second_factor_matrix,
    final_mapping_matrix,
    final_offset_vector,
    couple_tensor,
    feedforward_scaling_vector,
    feedforward_expand_matrix,
    feedforward_contract_matrix,
    upstream_sensitivity,
):
    aligned_number, shard_extent, features = alignment_tensor.shape
    channels = first_factor_matrix.shape[1]
    row_count, col_count, pair_width = couple_tensor.shape
    rows, cols = lax.axis_size("row"), lax.axis_size("col")
    ratio = rows // cols
    amino_number = row_count * rows
    normed_full, msa_hat, msa_inv = standardize_features(
        alignment_tensor.astype(F32), alignment_scaling_vector
    )
    normed = normed_full.astype(BF16)
    left_local = jnp.einsum(
        "srm,mc->rcs", normed, first_factor_matrix, preferred_element_type=F32
    ).astype(BF16)
    right_local = jnp.einsum(
        "srm,me->ers", normed, second_factor_matrix, preferred_element_type=F32
    ).astype(BF16)
    pairs = swap_pairs(rows, cols)
    right_moved = lax.ppermute(right_local, BOTH, pairs)
    left_rows = spread(left_local * (1.0 / aligned_number), "col").reshape(
        row_count * channels, aligned_number
    )
    right_blocks = spread(right_moved, "row")
    right_t = (
        right_blocks.reshape(cols, ratio, channels, shard_extent, aligned_number)
        .transpose(2, 1, 0, 3, 4)
        .reshape(channels * col_count, aligned_number)
    )
    result, grad, d_left, d_right, g_proj, g_expand, g_contract = pair_stage(
        left_rows,
        right_t,
        couple_tensor,
        upstream_sensitivity,
        final_mapping_matrix,
        feedforward_expand_matrix,
        feedforward_contract_matrix,
        final_offset_vector,
        feedforward_scaling_vector,
        shard_extent,
    )
    d_right = (
        d_right.reshape(ratio, cols, channels, shard_extent, aligned_number)
        .transpose(1, 0, 2, 3, 4)
        .reshape(rows, channels, shard_extent, aligned_number)
    )
    d_right = jnp.sum(exchange(d_right, "row").astype(F32), axis=0)
    d_right = lax.ppermute(d_right.astype(BF16), BOTH, pairs)
    d_left = d_left.reshape(cols, shard_extent, channels, aligned_number)
    d_left = jnp.sum(exchange(d_left, "col").astype(F32), axis=0).astype(BF16)

    left_weight = jnp.einsum("srm,rcs->cm", normed, d_left, preferred_element_type=F32)
    right_weight = jnp.einsum("srm,ers->em", normed, d_right, preferred_element_type=F32)
    d_normed = jnp.einsum("rcs,mc->srm", d_left, first_factor_matrix, preferred_element_type=F32)
    d_normed = d_normed + jnp.einsum(
        "ers,me->srm", d_right, second_factor_matrix, preferred_element_type=F32
    )
    alignment_sensitivity = standardize_reverse_mode(
        d_normed, msa_hat, msa_inv, alignment_scaling_vector
    ).astype(BF16)

    lanes = pair_width
    parts = [
        a.astype(BF16).reshape(-1, lanes)
        for a in (g_proj, g_expand, g_contract, left_weight, right_weight)
    ]
    sizes = [a.shape[0] for a in parts]
    devices = rows * cols
    mine = jnp.concatenate(parts, axis=0).reshape(devices, -1, lanes)
    mine = jnp.sum(exchange(mine, BOTH).astype(F32), axis=0) * (1.0 / amino_number)
    total = spread(mine.astype(BF16), BOTH).reshape(-1, lanes).astype(F32)
    at, outs = 0, []
    for size in sizes:
        outs.append(total[at : at + size])
        at += size
    t_proj, t_expand, t_contract, t_left, t_right = outs
    t_proj = t_proj.reshape(channels, channels, pair_width).transpose(1, 0, 2)
    return (
        result,
        grad,
        alignment_sensitivity,
        t_proj.reshape(channels * channels, pair_width),
        t_expand.T,
        t_contract,
        t_left.reshape(channels, features).T,
        t_right.reshape(channels, features).T,
    )


def solution(mesh):
    return jax.shard_map(
        on_device,
        mesh=mesh,
        in_specs=(
            P(None, ("row", "col"), None),
            P(),
            P(),
            P(),
            P(),
            P(),
            P("row", "col", None),
            P(),
            P(),
            P(),
            P("row", "col", None),
        ),
        out_specs=(
            P("row", "col", None),
            P("row", "col", None),
            P(None, ("row", "col"), None),
            P(),
            P(),
            P(),
            P(),
            P(),
        ),
        check_vma=False,
    )
```

time: 597 us -> 225 us (0.38)
  waiting for transfers between devices: 290 us -> 71.7 us
  local copies, waits for them, and re-layouts: 147 us -> 17.2 us
  matrix products: 98.2 us -> 4.23 us
  Pallas kernels: 0 us -> 68.3 us
  starting transfers between devices: 14.3 us -> 56.9 us
  loops' own time: 19 us -> 0 us
  between operations: 14.2 us -> 1.01 us
  other arithmetic: 11.1 us -> 4.85 us
    psum x1 -> x0, waiting for transfers between devices: 141 us -> none  [in_one(): so_far = lax.psum(ravelled, axis)]
    all_gather x2 -> x0, waiting for transfers between devices: 115 us -> none  [the longest x1 78.5 us: broadcast(): lax.all_gather(x, axis)]
    dot_general x102 -> x6, matrix products: 98.2 us -> 4.23 us  [the longest x1 1.57 us: on_device(): jnp.einsum('srm,me->ers', normed, second_factor_matrix, preferred_element...]
    pallas_call x0 -> x1, Pallas kernels: none -> 68.3 us  [pair_stage(): pl.pallas_call(pair_kernel, grid=(rows // block,), in_specs=[flat, whole(...]
    while x441 -> x0, local copies, waits for them, and re-layouts: 48.1 us -> none
    all_to_all x3 -> x6, starting transfers between devices: 14.2 us -> 55.6 us  [the longest x3 30.2 us: spread(): lax.all_to_all(jnp.broadcast_to(x[None], (count, *x.shape)), axis, 0, 0,...]
    all_to_all x3 -> x6, waiting for transfers between devices: 33.2 us -> 71.7 us  [the longest x3 37 us: exchange(): return lax.all_to_all(x, axis, 0, 0, tiled=True)]
    convert_element_type x17 -> x1, local copies, waits for them, and re-layouts: 32.6 us -> 0.18 us  [on_device(): total = spread(mine.astype(BF16), BOTH).reshape(-1, lanes).astype(F32)]
  transfers between devices with their start and end apart: 6 -> 8, of which waited for: 6 -> 6; matrix products, arithmetic and copies ran while one was open for 2% -> 5% of each run, Pallas kernels for 0% -> 0%
where the time goes in v1:
time: 225 us; the launch traced here: 224 us
  waiting for transfers between devices  71.7 us (32%)
  Pallas kernels  68.3 us (30%)
  starting transfers between devices  56.9 us (25%)
  local copies, waits for them, and re-layouts  17.2 us (8%)
  other arithmetic  4.85 us (2%)
  matrix products  4.23 us (2%)
    pallas_call x1, Pallas kernels, pair_stage(): pl.pallas_call(pair_kernel, grid=(rows // block,), in_specs=[flat, whole(...  68.3 us
    all_to_all x3, waiting for transfers between devices, exchange(): return lax.all_to_all(x, axis, 0, 0, tiled=True)  37 us
    all_to_all x3, waiting for transfers between devices, spread(): lax.all_to_all(jnp.broadcast_to(x[None], (count, *x.shape)), axis, 0, 0,...  34.7 us
    all_to_all x3, starting transfers between devices, spread(): lax.all_to_all(jnp.broadcast_to(x[None], (count, *x.shape)), axis, 0, 0,...  30.2 us
    all_to_all x3, starting transfers between devices, exchange(): return lax.all_to_all(x, axis, 0, 0, tiled=True)  25.4 us
  transfers between devices with their start and end apart: 8, of which 6 were waited for; matrix products, arithmetic and copies ran while one was open for 5% of the time, Pallas kernels for 0%

profile of v1, /device:TPU:1, one launch (start us, length us, event | category | flops | bytes accessed | tf_op | source)
XLA Modules:
  0.0 224.3 jit_solution(617001724760473384)
XLA Ops:
  0.6 1.3 convert_reduce_fusion.1
  1.9 1.4 fusion.17
  3.4 1.6 fusion.9
  5.7 1.2 broadcast_in_dim.11
  6.9 21.2 %all-to-all-start.1 = ((bf16[16,32,8,128]{3,2,1,0:T(8,128)(2,1)}), bf16[16,32,8,128]{3,2,1,0:T(8,128)(2,1)S(1)}, u32[]{:S(2)}, u32[]{:S(2)}) async-start(bf16[16,32,8,128]{3,2,1,0:T(8,128)(2,1)} %broadcast_in_dim.11), calls=%async_computation.1 | async-start | bytes 2097152 | tf_op jit(solution)/shard_map/all_to_all | solution.py:239
  28.6 16.7 %all-to-all-done.1 = bf16[16,32,8,128]{3,2,1,0:T(8,128)(2,1)S(1)} async-done(((bf16[16,32,8,128]{3,2,1,0:T(8,128)(2,1)}), bf16[16,32,8,128]{3,2,1,0:T(8,128)(2,1)S(1)}, u32[]{:S(2)}, u32[]{:S(2)}) %all-to-all-start.1) | async-done | bytes 1048608 | tf_op jit(solution)/shard_map/all_to_all | solution.py:239
  46.3 3.5 %all-to-all-start = ((bf16[8,8,32,128]{3,2,1,0:T(8,128)(2,1)}), bf16[8,8,32,128]{3,2,1,0:T(8,128)(2,1)S(1)}, u32[]{:S(2)}, u32[]{:S(2)}) async-start(bf16[8,8,32,128]{3,2,1,0:T(8,128)(2,1)} %broadcast_in_dim.10), calls=%async_computation | async-start | bytes 1048576 | tf_op jit(solution)/shard_map/all_to_all | solution.py:239
  52.3 1.3 copy.51
  53.6 5.2 %all-to-all-done = bf16[8,8,32,128]{3,2,1,0:T(8,128)(2,1)S(1)} async-done(((bf16[8,8,32,128]{3,2,1,0:T(8,128)(2,1)}), bf16[8,8,32,128]{3,2,1,0:T(8,128)(2,1)S(1)}, u32[]{:S(2)}, u32[]{:S(2)}) %all-to-all-start) | async-done | bytes 524320 | tf_op jit(solution)/shard_map/all_to_all | solution.py:239
  60.4 68.3 %pair_stage.1 = (bf16[64,128,128]{2,1,0:T(8,128)(2,1)}, bf16[64,128,128]{2,1,0:T(8,128)(2,1)}, bf16[2048,128]{1,0:T(8,128)(2,1)}, bf16[16,32,8,128]{3,2,1,0:T(8,...) custom-call(bf16[2048,128]{1,0:T(8,128)(2,1)} %bitcast.59, bf16[4096,128]{1,0:T(8,128)(2,1)} %bitcast.55, ...), custom_call_target="tpu_custom_call" | custom-call | tf_op jit(solution)/shard_map/pair_stage/pallas_call | solution.py:174
  128.7 3.5 %all-to-all-start.2 = ((bf16[8,8,32,128]{3,2,1,0:T(8,128)(2,1)}), bf16[8,8,32,128]{3,2,1,0:T(8,128)(2,1)S(1)}, u32[]{:S(2)}, u32[]{:S(2)}) async-start(bf16[8,8,32,128]{3,2,1,0:T(8,128)(2,1)} %bitcast.66), calls=%async_computation.2 | async-start | bytes 1048576 | tf_op jit(solution)/shard_map/all_to_all | solution.py:245
  132.2 2.4 %copy.56 = bf16[2,8,32,8,128]{4,3,2,0,1:T(8,128)(2,1)} copy(bf16[2,8,32,8,128]{4,3,2,1,0:T(8,128)(2,1)} %bitcast.62) | data formatting | bytes 2097152 | tf_op jit(solution)/shard_map/reshape | solution.py:310
  134.6 6.1 %all-to-all-done.2 = bf16[8,8,32,128]{3,2,1,0:T(8,128)(2,1)S(1)} async-done(((bf16[8,8,32,128]{3,2,1,0:T(8,128)(2,1)}), bf16[8,8,32,128]{3,2,1,0:T(8,128)(2,1)S(1)}, u32[]{:S(2)}, u32[]{:S(2)}) %all-to-all-start.2) | async-done | bytes 524320 | tf_op jit(solution)/shard_map/all_to_all | solution.py:245
  140.7 5.3 %all-to-all-start.3 = ((bf16[16,32,8,128]{3,2,1,0:T(8,128)(2,1)}), bf16[16,32,8,128]{3,2,1,0:T(8,128)(2,1)S(1)}, u32[]{:S(2)}, u32[]{:S(2)}) async-start(bf16[16,32,8,128]{3,2,1,0:T(8,128)(2,1)} %bitcast.17), calls=%async_computation.3 | async-start | bytes 2097152 | tf_op jit(solution)/shard_map/all_to_all | solution.py:245
  146.1 1.0 convert_dynamic-update-slice_fusion.2
  147.6 15.7 %all-to-all-done.3 = bf16[16,32,8,128]{3,2,1,0:T(8,128)(2,1)S(1)} async-done(((bf16[16,32,8,128]{3,2,1,0:T(8,128)(2,1)}), bf16[16,32,8,128]{3,2,1,0:T(8,128)(2,1)S(1)}, u32[]{:S(2)}, u32[]{:S(2)}) %all-to-all-start.3) | async-done | bytes 1048608 | tf_op jit(solution)/shard_map/all_to_all | solution.py:245
  164.7 1.1 reshape.103
  165.8 16.6 %all-to-all-start.4 = ((bf16[128,17,128]{2,1,0:T(8,128)(2,1)}), bf16[128,17,128]{2,1,0:T(8,128)(2,1)S(1)}, u32[]{:S(2)}, u32[]{:S(2)}) async-start(bf16[128,17,128]{2,1,0:T(8,128)(2,1)} %reshape.103), calls=%async_computation.4 | async-start | bytes 1572864 | tf_op jit(solution)/shard_map/all_to_all | solution.py:245
  182.8 15.2 %all-to-all-done.4 = bf16[128,17,128]{2,1,0:T(8,128)(2,1)S(1)} async-done(((bf16[128,17,128]{2,1,0:T(8,128)(2,1)}), bf16[128,17,128]{2,1,0:T(8,128)(2,1)S(1)}, u32[]{:S(2)}, u32[]{:S(2)}) %all-to-all-start.4) | async-done | bytes 557088 | tf_op jit(solution)/shard_map/all_to_all | solution.py:245
  198.2 1.0 broadcast_in_dim.14
  199.2 5.4 %all-to-all-start.5 = ((bf16[128,17,128]{2,1,0:T(8,128)(2,1)}), bf16[128,17,128]{2,1,0:T(8,128)(2,1)S(1)}, u32[]{:S(2)}, u32[]{:S(2)}) async-start(bf16[128,17,128]{2,1,0:T(8,128)(2,1)} %broadcast_in_dim.14), calls=%async_computation.5 | async-start | bytes 1572864 | tf_op jit(solution)/shard_map/all_to_all | solution.py:239
  206.3 1.1 copy.59
  207.4 12.7 %all-to-all-done.5 = bf16[128,17,128]{2,1,0:T(8,128)(2,1)S(1)} async-done(((bf16[128,17,128]{2,1,0:T(8,128)(2,1)}), bf16[128,17,128]{2,1,0:T(8,128)(2,1)S(1)}, u32[]{:S(2)}, u32[]{:S(2)}) %all-to-all-start.5) | async-done | bytes 557088 | tf_op jit(solution)/shard_map/all_to_all | solution.py:239
  222.4 1.1 copy.58
  (65 shorter events, 13.3 us)
Async XLA Ops:
  0.6 2.7 %copy-start = (bf16[256,32]{0,1:T(8,128)(2,1)S(1)}, bf16[256,32]{0,1:T(8,128)(2,1)}, u32[]{:S(2)}) copy-start(bf16[256,32]{0,1:T(8,128)(2,1)} %param.14) | copy-start | bytes 49156
  3.4 24.8 %copy-start.1 = (bf16[128,8,256]{2,1,0:T(8,128)(2,1)S(1)}, bf16[128,8,256]{2,1,0:T(8,128)(2,1)}, u32[]{:S(2)}) copy-start(bf16[128,8,256]{2,1,0:T(8,128)(2,1)} %param.11) | copy-start | bytes 1572868
  3.4 24.7 %copy-start.9 = (bf16[256,32]{0,1:T(8,128)(2,1)S(1)}, bf16[256,32]{0,1:T(8,128)(2,1)}, u32[]{:S(2)}) copy-start(bf16[256,32]{0,1:T(8,128)(2,1)} %param.13) | copy-start | bytes 49156
  3.4 24.7 %copy-start.10 = (f32[256]{0:T(256)S(1)}, f32[256]{0:T(256)}, u32[]{:S(2)}) copy-start(f32[256]{0:T(256)} %param.12) | copy-start | bytes 3076
  5.0 0.7 collective-permute-start
  6.9 42.9 %copy-start.4 = (bf16[128,512]{1,0:T(8,128)(2,1)S(1)}, bf16[128,512]{1,0:T(8,128)(2,1)}, u32[]{:S(2)}) copy-start(bf16[128,512]{1,0:T(8,128)(2,1)} %expand_ref.1) | copy-start | bytes 393220
  6.9 38.5 %all-to-all-start.1 = ((bf16[16,32,8,128]{3,2,1,0:T(8,128)(2,1)}), bf16[16,32,8,128]{3,2,1,0:T(8,128)(2,1)S(1)}, u32[]{:S(2)}, u32[]{:S(2)}) async-start(bf16[16,32,8,128]{3,2,1,0:T(8,128)(2,1)} %broadcast_in_dim.11), calls=%async_computation.1 | async-start | bytes 2097152 | tf_op jit(solution)/shard_map/all_to_all | solution.py:239
  28.1 22.4 %copy-start.5 = (bf16[512,128]{1,0:T(8,128)(2,1)S(1)}, bf16[512,128]{1,0:T(8,128)(2,1)}, u32[]{:S(2)}) copy-start(bf16[512,128]{1,0:T(8,128)(2,1)} %contract_ref.1) | copy-start | bytes 393220
  28.2 23.2 %copy-start.8 = (bf16[1024,128]{1,0:T(8,128)(2,1)S(1)}, bf16[1024,128]{1,0:T(8,128)(2,1)}, u32[]{:S(2)}) copy-start(bf16[1024,128]{1,0:T(8,128)(2,1)} %param.15) | copy-start | bytes 786436
  46.3 12.5 %all-to-all-start = ((bf16[8,8,32,128]{3,2,1,0:T(8,128)(2,1)}), bf16[8,8,32,128]{3,2,1,0:T(8,128)(2,1)S(1)}, u32[]{:S(2)}, u32[]{:S(2)}) async-start(bf16[8,8,32,128]{3,2,1,0:T(8,128)(2,1)} %broadcast_in_dim.10), calls=%async_computation | async-start | bytes 1048576 | tf_op jit(solution)/shard_map/all_to_all | solution.py:239
  49.8 9.0 %copy-start.11 = (f32[128]{0:T(128)S(1)}, f32[128]{0:T(128)}, u32[]{:S(2)}) copy-start(f32[128]{0:T(128)} %param.16) | copy-start | bytes 1540
  49.8 9.9 %copy-start.12 = (f32[128]{0:T(128)S(1)}, f32[128]{0:T(128)}, u32[]{:S(2)}) copy-start(f32[128]{0:T(128)} %param.18) | copy-start | bytes 1540
  51.4 9.0 %copy-start.2 = (bf16[32,32,128]{2,1,0:T(8,128)(2,1)}, bf16[32,32,128]{2,1,0:T(8,128)(2,1)S(1)}, u32[]{:S(2)}) copy-start(bf16[32,32,128]{2,1,0:T(8,128)(2,1)S(1)} %copy.52) | copy-start | bytes 786436
  58.8 1.6 copy-start.3
  128.7 12.0 %all-to-all-start.2 = ((bf16[8,8,32,128]{3,2,1,0:T(8,128)(2,1)}), bf16[8,8,32,128]{3,2,1,0:T(8,128)(2,1)S(1)}, u32[]{:S(2)}, u32[]{:S(2)}) async-start(bf16[8,8,32,128]{3,2,1,0:T(8,128)(2,1)} %bitcast.66), calls=%async_computation.2 | async-start | bytes 1048576 | tf_op jit(solution)/shard_map/all_to_all | solution.py:245
  132.2 13.8 %copy-start.6 = (f32[1024,128]{1,0:T(8,128)S(1)}, f32[1024,128]{1,0:T(8,128)}, u32[]{:S(2)}) copy-start(f32[1024,128]{1,0:T(8,128)} %get-tuple-element.19) | copy-start | bytes 1572868
  134.6 12.4 %copy-start.7 = (f32[512,128]{1,0:T(8,128)S(1)}, f32[512,128]{1,0:T(8,128)}, u32[]{:S(2)}) copy-start(f32[512,128]{1,0:T(8,128)} %get-tuple-element.21) | copy-start | bytes 786436
  140.7 22.7 %all-to-all-start.3 = ((bf16[16,32,8,128]{3,2,1,0:T(8,128)(2,1)}), bf16[16,32,8,128]{3,2,1,0:T(8,128)(2,1)S(1)}, u32[]{:S(2)}, u32[]{:S(2)}) async-start(bf16[16,32,8,128]{3,2,1,0:T(8,128)(2,1)} %bitcast.17), calls=%async_computation.3 | async-start | bytes 2097152 | tf_op jit(solution)/shard_map/all_to_all | solution.py:245
  163.5 0.7 collective-permute-start.1
  165.8 32.2 %all-to-all-start.4 = ((bf16[128,17,128]{2,1,0:T(8,128)(2,1)}), bf16[128,17,128]{2,1,0:T(8,128)(2,1)S(1)}, u32[]{:S(2)}, u32[]{:S(2)}) async-start(bf16[128,17,128]{2,1,0:T(8,128)(2,1)} %reshape.103), calls=%async_computation.4 | async-start | bytes 1572864 | tf_op jit(solution)/shard_map/all_to_all | solution.py:245
  199.2 21.0 %all-to-all-start.5 = ((bf16[128,17,128]{2,1,0:T(8,128)(2,1)}), bf16[128,17,128]{2,1,0:T(8,128)(2,1)S(1)}, u32[]{:S(2)}, u32[]{:S(2)}) async-start(bf16[128,17,128]{2,1,0:T(8,128)(2,1)} %broadcast_in_dim.14), calls=%async_computation.5 | async-start | bytes 1572864 | tf_op jit(solution)/shard_map/all_to_all | solution.py:239

commit v2 on v1

v2 whole, which is shorter than its diff:
```python
import jax
import jax.numpy as jnp
from jax import lax
from jax.experimental import pallas as pl
from jax.experimental.pallas import tpu as pltpu
from jax.sharding import PartitionSpec as P

EPSILON = 1e-05
ROOT_HALF = 0.7071067811865476
INV_ROOT_TWO_PI = 0.3989422804014327

F32 = jnp.float32
BF16 = jnp.bfloat16
CHUNK = 128
BOTH = ("row", "col")


def matmul(a, b):
    return lax.dot_general(a, b, (((1,), (0,)), ((), ())), preferred_element_type=F32)


def matmul_nt(a, b):
    return lax.dot_general(a, b, (((1,), (1,)), ((), ())), preferred_element_type=F32)


def standardize_features(values, gain_vec):
    average = jnp.mean(values, axis=-1, keepdims=True)
    centred = values - average
    variance = jnp.mean(centred * centred, axis=-1, keepdims=True)
    inv_scale = lax.rsqrt(variance + EPSILON)
    vhat_values = centred * inv_scale
    return (vhat_values * gain_vec, vhat_values, inv_scale)


def standardize_reverse_mode(incoming, vhat_values, inv_scale, gain_vec):
    scaled = incoming * gain_vec
    return inv_scale * (
        scaled
        - jnp.mean(scaled, axis=-1, keepdims=True)
        - vhat_values * jnp.mean(scaled * vhat_values, axis=-1, keepdims=True)
    )


def pair_kernel(
    core_ref,
    left_ref,
    own_ref,
    other_ref,
    pair_ref,
    cot_ref,
    proj_ref,
    proj_t_ref,
    expand_ref,
    expand_t_ref,
    contract_ref,
    contract_t_ref,
    offset_ref,
    gain_ref,
    result_ref,
    grad_ref,
    d_left_ref,
    own_out_ref,
    other_out_ref,
    right_t_scr,
    right_scr,
    outer_scr,
    d_outer_scr,
    acc_right,
    hidden_scr,
    d_hidden_scr,
    acc_left,
    left_t_scr,
    g_proj_ref,
    g_expand_ref,
    g_contract_ref,
):
    step = pl.program_id(0)
    first = core_ref[0] == 0
    block = pair_ref.shape[0]
    seqs = left_ref.shape[1]
    wide = right_t_scr.shape[0]
    width = proj_t_ref.shape[0]
    lanes = pair_ref.shape[1]
    channels = wide // lanes
    rows = block * channels
    blocks = left_ref.shape[0] // rows
    chunk = 2 * lanes
    early = rows - 2 * channels

    def left_rows(b, start, size):
        return left_ref[pl.ds(pl.multiple_of(b * rows + start, 2 * channels), size), :]

    def outer_product(b, start, stop, at):
        outer_scr[start:stop, at] = matmul(left_rows(b, start, stop - start), right_scr[:, at]).astype(BF16)

    def pieces(h):
        each = wide // (4 * chunk)
        return [slice((h * each + k) * chunk, (h * each + k + 1) * chunk) for k in range(each)]

    def backward(b, h):
        at = slice(h * wide // 4, (h + 1) * wide // 4)
        part = matmul(d_outer_scr[:, at], right_t_scr[at, :])
        left_t = left_t_scr[...]
        for to in pieces(h):
            acc_right[:, to] += matmul(left_t, d_outer_scr[:, to])
        if h == 0:
            acc_left[...] = part
        elif h < 3:
            acc_left[...] += part
        else:
            total = (acc_left[...] + part) * (1.0 / seqs)
            d_left_ref[pl.ds(pl.multiple_of(b * rows, rows), rows), :] = total.astype(BF16)

    @pl.when(step == 0)
    def _():
        for e in range(channels):
            at = slice(e * lanes, (e + 1) * lanes)
            own, other = own_ref[:, e], other_ref[:, e]
            both = (jnp.where(first, own, other), jnp.where(first, other, own))
            tile = jnp.stack(both, axis=1).reshape(lanes, seqs)
            right_t_scr[at, :] = tile
            right_scr[:, at] = tile.T
        acc_right[...] = jnp.zeros_like(acc_right)
        d_outer_scr[...] = jnp.zeros_like(d_outer_scr)
        g_proj_ref[...] = jnp.zeros_like(g_proj_ref)
        g_expand_ref[...] = jnp.zeros_like(g_expand_ref)
        g_contract_ref[...] = jnp.zeros_like(g_contract_ref)
        for h in range(4):
            for at in pieces(h):
                outer_product(0, 0, early, at)

    before = jnp.maximum(step - 1, 0)
    after = jnp.minimum(step + 1, blocks - 1)
    left_t_scr[...] = left_rows(before, 0, rows).T

    gain = jnp.broadcast_to(gain_ref[...], (2 * lanes, width)).T
    offset = jnp.broadcast_to(offset_ref[...], (2 * lanes, width)).T

    def columns(scr, i, some):
        row = slice(i * channels, (i + 1) * channels)
        tiles = [
            scr[row, e * lanes : (e + 1) * lanes] for e in range(some.start, some.stop)
        ]
        return jnp.concatenate(tiles, axis=0)

    def beside(ref, i):
        return jnp.concatenate([ref[i].T, ref[i + 1].T], axis=1)

    scale = 1.0 / width

    def forward(p):
        i = 2 * p
        outer = jnp.concatenate([columns(outer_scr, i + k, slice(0, channels)) for k in range(2)], axis=1)
        update = matmul(proj_t_ref[...], outer) + offset
        middle = (beside(pair_ref, i).astype(F32) + update).astype(BF16).astype(F32)
        average = jnp.sum(middle, axis=0, keepdims=True) * scale
        centred = middle - average
        variance = jnp.sum(centred * centred, axis=0, keepdims=True) * scale
        inv = lax.rsqrt(variance + EPSILON)
        vhat = centred * inv
        normed = (vhat * gain).astype(BF16)
        return dict(p=p, middle=middle, vhat=vhat, inv=inv, normed=normed,
                    cot=beside(cot_ref, i))

    def activate(st, h):
        p = st["p"]
        at = slice(h * CHUNK, (h + 1) * CHUNK)
        pre = matmul(expand_t_ref[at, :], st["normed"])
        half = 0.5 + 0.5 * lax.erf(pre * ROOT_HALF)
        hidden_scr[p, at, :] = (pre * half).astype(BF16)
        slope = half + pre * jnp.exp(-0.5 * pre * pre) * INV_ROOT_TWO_PI
        d_hidden_scr[p, at, :] = (matmul(contract_ref[at, :], st["cot"]) * slope).astype(BF16)

    def through(st):
        p, i = st["p"], 2 * st["p"]
        cot, vhat = st["cot"], st["vhat"]
        q = matmul(expand_ref[...], d_hidden_scr[p]) * gain
        result = (st["middle"] + matmul(contract_t_ref[...], hidden_scr[p])).astype(BF16)
        result_ref[i] = result[:, :lanes].T
        result_ref[i + 1] = result[:, lanes:].T
        q_mean = jnp.sum(q, axis=0, keepdims=True) * scale
        q_hat = jnp.sum(q * vhat, axis=0, keepdims=True) * scale
        grad = (cot.astype(F32) + st["inv"] * (q - q_mean - vhat * q_hat)).astype(BF16)
        grad_ref[i] = grad[:, :lanes].T
        grad_ref[i + 1] = grad[:, lanes:].T
        st["grad"] = grad

    def weigh(st, h):
        p, i = st["p"], 2 * st["p"]
        part = proj_ref.shape[0] // 4
        at = slice(h * part, (h + 1) * part)
        d_outer = matmul(proj_ref[at, :], st["grad"]).astype(BF16)
        for k in range(2):
            row = slice((i + k) * channels, (i + k + 1) * channels)
            for e in range(part // channels):
                to = h * (part // channels) + e
                d_outer_scr[row, to * lanes : (to + 1) * lanes] = d_outer[
                    e * channels : (e + 1) * channels, k * lanes : (k + 1) * lanes
                ]
        some = slice(h * part // channels, (h + 1) * part // channels)
        outer = jnp.concatenate(
            [columns(outer_scr, i, some), columns(outer_scr, i + 1, some)], axis=1
        )
        g_proj_ref[at, :] += matmul_nt(outer, st["grad"])
        at = slice(h * CHUNK, (h + 1) * CHUNK)
        g_contract_ref[at, :] += matmul_nt(hidden_scr[p, at, :], st["cot"])
        g_expand_ref[at, :] += matmul_nt(d_hidden_scr[p, at, :], st["normed"])

    last = None
    count = block // 2
    for p in range(count + 1):
        now = forward(p) if p < count else None
        if last is not None:
            through(last)
        for h in range(4):
            if now is not None:
                activate(now, h)
            if last is not None:
                weigh(last, h)
            if p == 0:
                for at in pieces(h):
                    outer_product(step, early, rows, at)
                backward(before, h)
            if p == count:
                for at in pieces(h):
                    outer_product(after, 0, early, at)
        last = now

    @pl.when(step == pl.num_programs(0) - 1)
    def _():
        left_t_scr[...] = left_rows(step, 0, rows).T
        for h in range(4):
            backward(step, h)
        each = own_ref.shape[2]
        halves = own_ref.shape[0]

        def hand_out(at, even, odd):
            own_out_ref[:, at, :] = jnp.where(first, even, odd).astype(BF16)
            other_out_ref[:, at, :] = jnp.where(first, odd, even).astype(BF16)

        for e in range(channels):
            tile = acc_right[:, e * lanes : (e + 1) * lanes].T.reshape(halves, 2, each, seqs)
            hand_out(slice(e * each, (e + 1) * each), tile[:, 0], tile[:, 1])

        def weight_rows(k):
            full = width
            per = full // channels
            if k < channels // per:
                cs = range(k * per, (k + 1) * per)
                return jnp.concatenate(
                    [g_proj_ref[pl.ds(c, channels, stride=channels), :] for c in cs], axis=0
                )
            k -= channels // per
            at = slice(k * full, (k + 1) * full)
            if k < g_expand_ref.shape[0] // full:
                return g_expand_ref[at, :].T
            at = slice(at.start - g_expand_ref.shape[0], at.stop - g_expand_ref.shape[0])
            return g_contract_ref[at, :]

        base = channels * each
        for m in range(halves):
            even, odd = weight_rows(2 * m), weight_rows(2 * m + 1)
            own_out_ref[m, base:, :] = jnp.where(first, even, odd).astype(BF16)
            other_out_ref[m, base:, :] = jnp.where(first, odd, even).astype(BF16)


def pair_stage(core, left, own, other, pair, cot, proj, expand, contract, offset, gain):
    each = own.shape[2]
    rows, lanes, width = pair.shape
    seqs = left.shape[1]
    channels = own.shape[1]
    wide = channels * lanes
    hidden = expand.shape[1]
    block = 8
    by_e = (
        proj.reshape(channels, channels, width).transpose(1, 0, 2).reshape(channels * channels, width)
    )
    whole = lambda shape: pl.BlockSpec(shape, lambda b: (0,) * len(shape))
    weights = channels * channels + 2 * hidden
    parts = (own.shape[0], channels * each + weights // (2 * own.shape[0]), width)
    tiles = pl.BlockSpec((block, lanes, width), lambda b: (b, 0, 0))
    flat = whole((rows * channels, seqs))
    return pl.pallas_call(
        pair_kernel,
        grid=(rows // block,),
        in_specs=[
            pl.BlockSpec(memory_space=pltpu.SMEM),
            flat,
            whole(own.shape),
            whole(own.shape),
            tiles,
            tiles,
            whole((channels * channels, width)),
            whole((width, channels * channels)),
            whole((width, hidden)),
            whole((hidden, width)),
            whole((hidden, width)),
            whole((width, hidden)),
            whole((1, width)),
            whole((1, width)),
        ],
        out_specs=[
            tiles,
            tiles,
            flat,
            whole(parts),
            whole(parts),
        ],
        out_shape=[
            jax.ShapeDtypeStruct((rows, lanes, width), BF16),
            jax.ShapeDtypeStruct((rows, lanes, width), BF16),
            jax.ShapeDtypeStruct((rows * channels, seqs), BF16),
            jax.ShapeDtypeStruct(parts, BF16),
            jax.ShapeDtypeStruct(parts, BF16),
        ],
        scratch_shapes=[
            pltpu.VMEM((wide, seqs), BF16),
            pltpu.VMEM((seqs, wide), BF16),
            pltpu.VMEM((block * channels, wide), BF16),
            pltpu.VMEM((block * channels, wide), BF16),
            pltpu.VMEM((seqs, wide), F32),
            pltpu.VMEM((block // 2, hidden, 2 * lanes), BF16),
            pltpu.VMEM((block // 2, hidden, 2 * lanes), BF16),
            pltpu.VMEM((block * channels, seqs), F32),
            pltpu.VMEM((seqs, block * channels), BF16),
            pltpu.VMEM((channels * channels, width), F32),
            pltpu.VMEM((hidden, width), F32),
            pltpu.VMEM((hidden, width), F32),
        ],
        compiler_params=pltpu.CompilerParams(
            dimension_semantics=("arbitrary",), vmem_limit_bytes=56 * 1024 * 1024
        ),
        name="pair_stage",
    )(
        core,
        left,
        own,
        other,
        pair,
        cot,
        by_e,
        by_e.T,
        expand,
        expand.T,
        contract,
        contract.T,
        offset.astype(F32)[None, :],
        gain.astype(F32)[None, :],
    )


def unpack_kernel(
    core_ref, own_ref, other_ref, scale_ref, proj_ref, expand_ref, contract_ref, left_ref, right_ref
):
    first = core_ref[0] == 0
    size = own_ref.shape[2]
    scale = scale_ref[0]
    halves = own_ref.shape[0] - 1

    def chunk(k):
        own, other = own_ref[1 + k // 2].astype(F32), other_ref[1 + k // 2].astype(F32)
        picked = jnp.where(first, own, other) if k % 2 == 0 else jnp.where(first, other, own)
        return picked * scale

    at = 0
    for k in range(proj_ref.shape[0] // size):
        proj_ref[k * size : (k + 1) * size, :] = chunk(at)
        at += 1
    for k in range(expand_ref.shape[1] // size):
        expand_ref[:, k * size : (k + 1) * size] = chunk(at)
        at += 1
    for k in range(contract_ref.shape[0] // size):
        contract_ref[k * size : (k + 1) * size, :] = chunk(at)
        at += 1
    factors = ((own_ref[0].astype(F32) + other_ref[0].astype(F32)) * scale).T
    channels = left_ref.shape[1]
    for h in range(left_ref.shape[0] // size):
        rows = slice(h * size, (h + 1) * size)
        left_ref[rows, :] = factors[:, 2 * h * channels : (2 * h + 1) * channels]
        right_ref[rows, :] = factors[:, (2 * h + 1) * channels : (2 * h + 2) * channels]


def unpack(core, own, other, scale, shapes):
    smem = pl.BlockSpec(memory_space=pltpu.SMEM)
    vmem = pl.BlockSpec(memory_space=pltpu.VMEM)
    return pl.pallas_call(
        unpack_kernel,
        in_specs=[smem, vmem, vmem, smem],
        out_specs=[vmem] * len(shapes),
        out_shape=[jax.ShapeDtypeStruct(shape, F32) for shape in shapes],
        name="unpack",
    )(core, own, other, jnp.full((1,), scale, F32))


def parity_groups():
    rows = lax.axis_size("row")
    return [list(range(k, rows, 2)) for k in range(2)]


def exchange(x, axis):
    groups = parity_groups() if axis == "row" else None
    return lax.all_to_all(x, axis, 0, 0, tiled=True, axis_index_groups=groups)


def spread(x, axis):
    count = lax.axis_size("row") // 2 if axis == "row" else lax.axis_size(axis)
    return exchange(jnp.broadcast_to(x[None], (count, *x.shape)), axis)


def from_partner(x):
    return lax.ppermute(x, "row", [(k, k ^ 1) for k in range(lax.axis_size("row"))])


def summed(x):
    return jnp.sum(x.astype(F32), axis=0).astype(BF16)


def column_pairs(rows, cols):
    there = [(b, (b % rows) * cols + b // rows) for b in range(rows * cols)]
    return there, [(to, at) for at, to in there]


def on_device(
    alignment_tensor,
    alignment_scaling_vector,
    first_factor_matrix,
    second_factor_matrix,
    final_mapping_matrix,
    final_offset_vector,
    couple_tensor,
    feedforward_scaling_vector,
    feedforward_expand_matrix,
    feedforward_contract_matrix,
    upstream_sensitivity,
):
    aligned_number, shard_extent, features = alignment_tensor.shape
    channels = first_factor_matrix.shape[1]
    row_count, col_count, pair_width = couple_tensor.shape
    rows, cols = lax.axis_size("row"), lax.axis_size("col")
    amino_number = row_count * rows
    normed_full, msa_hat, msa_inv = standardize_features(
        alignment_tensor.astype(F32), alignment_scaling_vector
    )
    normed = normed_full.astype(BF16)
    left_local = jnp.einsum(
        "srm,mc->rcs", normed, first_factor_matrix, preferred_element_type=F32
    ).astype(BF16)
    right_local = jnp.einsum(
        "srm,me->ers", normed, second_factor_matrix, preferred_element_type=F32
    ).astype(BF16)
    there, back = column_pairs(rows, cols)
    right_moved = lax.ppermute(right_local, BOTH, there)
    left_rows = spread(left_local * (1.0 / aligned_number), "col")
    right_moved, left_rows = lax.optimization_barrier((right_moved, left_rows))
    own = spread(right_moved, "row")
    other = from_partner(own)
    core = (lax.axis_index("row") % 2).astype(jnp.int32)[None]
    result, grad, d_left, mine, theirs = pair_stage(
        core,
        left_rows.reshape(row_count * channels, aligned_number),
        own,
        other,
        couple_tensor,
        upstream_sensitivity,
        final_mapping_matrix,
        feedforward_expand_matrix,
        feedforward_contract_matrix,
        final_offset_vector,
        feedforward_scaling_vector,
    )
    lanes = pair_width
    mine = (mine.astype(F32) + from_partner(theirs).astype(F32)).astype(BF16)
    mine = summed(exchange(mine, "row"))
    size = channels * shard_extent
    d_right = mine[:size].reshape(channels, shard_extent, aligned_number)
    with_left = jnp.concatenate(
        [d_left.reshape(cols, size, lanes), mine[size:].reshape(cols, -1, lanes)], axis=1
    )
    d_right, with_left = lax.optimization_barrier((d_right, with_left))
    d_right = lax.ppermute(d_right, BOTH, back)
    with_left = summed(exchange(with_left, "col"))
    d_left = with_left[:size].reshape(shard_extent, channels, aligned_number)
    weights = with_left[size:]

    left_weight = jnp.einsum("srm,rcs->cm", normed, d_left, preferred_element_type=F32)
    right_weight = jnp.einsum("srm,ers->em", normed, d_right, preferred_element_type=F32)
    d_normed = jnp.einsum("rcs,mc->srm", d_left, first_factor_matrix, preferred_element_type=F32)
    d_normed = d_normed + jnp.einsum(
        "ers,me->srm", d_right, second_factor_matrix, preferred_element_type=F32
    )
    alignment_sensitivity = standardize_reverse_mode(
        d_normed, msa_hat, msa_inv, alignment_scaling_vector
    ).astype(BF16)

    factors = jnp.concatenate(
        [
            weight[:, k : k + lanes].astype(BF16)
            for k in range(0, features, lanes)
            for weight in (left_weight, right_weight)
        ],
        axis=0,
    )
    count = factors.shape[0]
    gathered = spread(jnp.concatenate([factors, weights], axis=0), "col")
    factors = summed(gathered[:, :count])
    weights = gathered[:, count:].reshape(-1, lanes)
    gathered = spread(jnp.stack([factors, weights], axis=0), "row")
    half = jnp.concatenate([summed(gathered[:, 0])[None], gathered[:, 1]], axis=0)
    outs = unpack(
        core,
        half,
        from_partner(half),
        1.0 / amino_number,
        (
            final_mapping_matrix.shape,
            feedforward_expand_matrix.shape,
            feedforward_contract_matrix.shape,
            first_factor_matrix.shape,
            second_factor_matrix.shape,
        ),
    )
    return (result, grad, alignment_sensitivity, *outs)


def solution(mesh):
    return jax.shard_map(
        on_device,
        mesh=mesh,
        in_specs=(
            P(None, ("row", "col"), None),
            P(),
            P(),
            P(),
            P(),
            P(),
            P("row", "col", None),
            P(),
            P(),
            P(),
            P("row", "col", None),
        ),
        out_specs=(
            P("row", "col", None),
            P("row", "col", None),
            P(None, ("row", "col"), None),
            P(),
            P(),
            P(),
            P(),
            P(),
        ),
        check_vma=False,
    )
```

time: 225 us -> 174 us (0.77)
  waiting for transfers between devices: 71.7 us -> 17.7 us
  blocking collectives: 0 us -> 49.8 us
  starting transfers between devices: 56.9 us -> 31.6 us
  Pallas kernels: 68.3 us -> 52.8 us
  local copies, waits for them, and re-layouts: 17.2 us -> 10.3 us
    all_to_all x6 -> x3, waiting for transfers between devices: 71.7 us -> 7.77 us  [exchange(): return lax.all_to_all(x, axis, 0, 0, tiled=True, axis_index_groups=groups)]
    all_to_all x0 -> x3, blocking collectives: none -> 49.8 us  [exchange(): return lax.all_to_all(x, axis, 0, 0, tiled=True, axis_index_groups=groups)]
    all_to_all x6 -> x3, starting transfers between devices: 55.6 us -> 13.8 us  [exchange(): return lax.all_to_all(x, axis, 0, 0, tiled=True, axis_index_groups=groups)]
    ppermute x2 -> x5, starting transfers between devices: 1.33 us -> 17.8 us  [the longest x3 6.83 us: from_partner(): lax.ppermute(x, 'row', [(k, k ^ 1) for k in range(lax.axis_size('row'))])]
    pallas_call x1 -> x2, Pallas kernels: 68.3 us -> 52.8 us  [the longest x1 50.5 us: pair_stage(): pl.pallas_call(pair_kernel, grid=(rows // block,), in_specs=[pl.BlockSpec...]
    ppermute x2 -> x5, waiting for transfers between devices: 0.01 us -> 9.94 us  [the longest x1 4.04 us: on_device(): right_moved = lax.ppermute(right_local, BOTH, there)]
    reshape x6 -> x1, local copies, waits for them, and re-layouts: 4.74 us -> 0.01 us  [on_device(): d_right = mine[:size].reshape(channels, shard_extent, aligned_number)]
    unnamed x31 -> x37, local copies, waits for them, and re-layouts: 3.52 us -> 7.4 us
  transfers between devices with their start and end apart: 8 -> 8, of which waited for: 6 -> 4; matrix products, arithmetic and copies ran while one was open for 5% -> 4% of each run, Pallas kernels for 0% -> 0%
where the time goes in v2:
time: 174 us; the launch traced here: 173 us
  Pallas kernels  52.8 us (30%)
  blocking collectives  49.8 us (29%)
  starting transfers between devices  31.6 us (18%)
  waiting for transfers between devices  17.7 us (10%)
  local copies, waits for them, and re-layouts  10.3 us (6%)
  other arithmetic  5.9 us (3%)
  matrix products  4.21 us (2%)
    pallas_call x1, Pallas kernels, pair_stage(): pl.pallas_call(pair_kernel, grid=(rows // block,), in_specs=[pl.BlockSpec...  50.5 us
    all_to_all x3, blocking collectives, exchange(): return lax.all_to_all(x, axis, 0, 0, tiled=True, axis_index_groups=groups)  49.8 us
    all_to_all x3, starting transfers between devices, exchange(): return lax.all_to_all(x, axis, 0, 0, tiled=True, axis_index_groups=groups)  13.8 us
    all_to_all x3, waiting for transfers between devices, exchange(): return lax.all_to_all(x, axis, 0, 0, tiled=True, axis_index_groups=groups)  7.77 us
    unnamed x37, local copies, waits for them, and re-layouts  7.4 us
    ppermute x3, starting transfers between devices, from_partner(): lax.ppermute(x, 'row', [(k, k ^ 1) for k in range(lax.axis_size('row'))])  6.83 us
    ppermute x1, starting transfers between devices, on_device(): right_moved = lax.ppermute(right_local, BOTH, there)  6.05 us
    ppermute x1, starting transfers between devices, on_device(): d_right = lax.ppermute(d_right, BOTH, back)  4.87 us
  transfers between devices with their start and end apart: 8, of which 4 were waited for; matrix products, arithmetic and copies ran while one was open for 4% of the time, Pallas kernels for 0%

profile of v2, /device:TPU:1, one launch (start us, length us, event | category | flops | bytes accessed | tf_op | source)
XLA Modules:
  0.0 173.3 jit_solution(10023484538680200408)
XLA Ops:
  0.6 1.3 convert_reduce_fusion
  1.9 1.4 fusion.17
  3.4 1.6 fusion.9
  5.8 6.2 %all-to-all-start = ((bf16[8,8,32,128]{3,2,1,0:T(8,128)(2,1)}), bf16[8,8,32,128]{3,2,1,0:T(8,128)(2,1)S(1)}, u32[]{:S(2)}, u32[]{:S(2)}) async-start(bf16[8,8,32,128]{3,2,1,0:T(8,128)(2,1)} %broadcast_in_dim.17), calls=%async_computation | async-start | bytes 1048576 | tf_op jit(solution)/shard_map/all_to_all | solution.py:402
  12.5 6.1 %collective-permute-start = (bf16[32,8,128]{2,0,1:T(8,128)(2,1)S(1)}, bf16[32,8,128]{2,0,1:T(8,128)(2,1)S(1)}, u32[]{:S(2)}, u32[]{:S(2)}) collective-permute-start(bf16[32,8,128]{2,0,1:T(8,128)(2,1)S(1)} %fusion.7), channel_id=1, source_target_pairs={{0,0},{1,8},{2,16},{3,24},{4,32},{5,40},{6,48},{7,56},{8,64},{9,72... | collective-permute-start | bytes 196616 | tf_op jit(solution)/shard_map/ppermute | solution.py:452
  18.6 4.0 %collective-permute-done = bf16[32,8,128]{2,0,1:T(8,128)(2,1)S(1)} collective-permute-done((bf16[32,8,128]{2,0,1:T(8,128)(2,1)S(1)}, bf16[32,8,128]{2,0,1:T(8,128)(2,1)S(1)}, u32[]{:S(2)}, u32[]{:S(2)}) %collective-permute-start) | collective-permute-done | bytes 65568 | tf_op jit(solution)/shard_map/ppermute | solution.py:452
  22.8 18.6 %all_to_all.30.own_ref = bf16[8,32,8,128]{3,2,1,0:T(8,128)(2,1)S(1)} all-to-all(bf16[8,32,8,128]{3,2,1,0:T(8,128)(2,1)S(1)} %broadcast_in_dim.18), channel_id=1, replica_groups={{0,16,32,48,64,80,96,112},{8,24,40,56,72,88,104,120},{1,17,33,49,65,81,..., dimensions={0} | all-to-all | bytes 1048576 | tf_op jit(solution)/shard_map/all_to_all | solution.py:402
  41.4 2.1 %collective-permute-start.1 = (bf16[8,32,8,128]{3,2,1,0:T(8,128)(2,1)S(1)}, bf16[8,32,8,128]{3,2,1,0:T(8,128)(2,1)S(1)}, u32[]{:S(2)}, u32[]{:S(2)}) collective-permute-start(bf16[8,32,8,128]{3,2,1,0:T(8,128)(2,1)S(1)} %all_to_all.30.own_ref), channel_id=1, source_target_pairs={{0,8},{8,0},{16,24},{24,16},{32,40},{40,32},{48,56},{56,48},{64,72... | collective-permute-start | bytes 1572872 | tf_op jit(solution)/shard_map/ppermute | solution.py:411
  46.8 50.5 %pair_stage.1 = (bf16[64,128,128]{2,1,0:T(8,128)(2,1)}, bf16[64,128,128]{2,1,0:T(8,128)(2,1)}, bf16[2048,128]{1,0:T(8,128)(2,1)}, bf16[8,384,128]{2,1,0:T(8,128)(2,1)}, bf16[8,384,128]{2,1,0:T(8,128)(2,1)}) custom-call(s32[1]{0:T(128)} %bitcast.core_ref, bf16[2048,128]{1,0:T(8,128)(2,1)} %bitcast.55, bf16[8,32,8,128]{3,2,1,0:T(8,128)(2,1)} %copy-done.4, ...), custom_call_target="tpu_custom_call" | custom-call | tf_op jit(solution)/shard_map/pair_stage/pallas_call | solution.py:283
  97.5 2.4 %collective-permute-done.2 = bf16[8,384,128]{2,1,0:T(8,128)(2,1)S(1)} collective-permute-done((bf16[8,384,128]{2,1,0:T(8,128)(2,1)}, bf16[8,384,128]{2,1,0:T(8,128)(2,1)S(1)}, u32[]{:S(2)}, u32[]{:S(2)}) %collective-permute-start.2) | collective-permute-done | bytes 786464 | tf_op jit(solution)/shard_map/ppermute | solution.py:411
  99.9 1.3 add_convert_fusion
  101.3 17.1 %all_to_all.31 = bf16[8,384,128]{2,1,0:T(8,128)(2,1)S(1)} all-to-all(bf16[8,384,128]{2,1,0:T(8,128)(2,1)S(1)} %add_convert_fusion), channel_id=1, replica_groups={{0,16,32,48,64,80,96,112},{8,24,40,56,72,88,104,120},{1,17,33,49,65,81,..., dimensions={0} | all-to-all | bytes 1572864 | tf_op jit(solution)/shard_map/all_to_all | solution.py:402
  119.4 3.5 %all-to-all-start.3 = ((bf16[8,272,128]{2,1,0:T(8,128)(2,1)}), bf16[8,272,128]{2,1,0:T(8,128)(2,1)S(1)}, u32[]{:S(2)}, u32[]{:S(2)}) async-start(bf16[8,272,128]{2,1,0:T(8,128)(2,1)} %pad_maximum_fusion), calls=%async_computation.3 | async-start | bytes 1114112 | tf_op jit(solution)/shard_map/all_to_all | solution.py:402
  122.9 4.9 %collective-permute-start.3 = (bf16[32,8,128]{2,0,1:T(8,128)(2,1)S(1)}, bf16[32,8,128]{2,0,1:T(8,128)(2,1)S(1)}, u32[]{:S(2)}, u32[]{:S(2)}) collective-permute-start(bf16[32,8,128]{2,0,1:T(8,128)(2,1)S(1)} %copy.53), channel_id=1, source_target_pairs={{0,0},{8,1},{16,2},{24,3},{32,4},{40,5},{48,6},{56,7},{64,8},{72,9... | collective-permute-start | bytes 196616 | tf_op jit(solution)/shard_map/ppermute | solution.py:480
  127.8 3.5 %collective-permute-done.3 = bf16[32,8,128]{2,0,1:T(8,128)(2,1)S(1)} collective-permute-done((bf16[32,8,128]{2,0,1:T(8,128)(2,1)S(1)}, bf16[32,8,128]{2,0,1:T(8,128)(2,1)S(1)}, u32[]{:S(2)}, u32[]{:S(2)}) %collective-permute-start.3) | collective-permute-done | bytes 65568 | tf_op jit(solution)/shard_map/ppermute | solution.py:480
  132.4 14.2 %all_to_all.32 = bf16[8,144,128]{2,1,0:T(8,128)(2,1)S(1)} all-to-all(bf16[8,144,128]{2,1,0:T(8,128)(2,1)S(1)} %broadcast_in_dim.21), channel_id=1, replica_groups=mesh['row'=16,'col'=8] {'col'}, dimensions={0} | all-to-all | bytes 589824 | tf_op jit(solution)/shard_map/all_to_all | solution.py:402
  147.5 4.1 %all-to-all-start.5 = ((bf16[8,2,128,128]{3,2,1,0:T(8,128)(2,1)}), bf16[8,2,128,128]{3,2,1,0:T(8,128)(2,1)S(1)}, u32[]{:S(2)}, u32[]{:S(2)}) async-start(bf16[8,2,128,128]{3,2,1,0:T(8,128)(2,1)} %broadcast_in_dim.22), calls=%async_computation.5 | async-start | bytes 1048576 | tf_op jit(solution)/shard_map/all_to_all | solution.py:402
  152.0 0.9 fusion.27
  152.9 7.8 %all-to-all-done.5 = bf16[8,2,128,128]{3,2,1,0:T(8,128)(2,1)S(1)} async-done(((bf16[8,2,128,128]{3,2,1,0:T(8,128)(2,1)}), bf16[8,2,128,128]{3,2,1,0:T(8,128)(2,1)S(1)}, u32[]{:S(2)}, u32[]{:S(2)}) %all-to-all-start.5) | async-done | bytes 524320 | tf_op jit(solution)/shard_map/all_to_all | solution.py:402
  160.8 4.6 %collective-permute-start.4 = (bf16[9,128,128]{2,1,0:T(8,128)(2,1)S(1)}, bf16[9,128,128]{2,1,0:T(8,128)(2,1)S(1)}, u32[]{:S(2)}, u32[]{:S(2)}) collective-permute-start(bf16[9,128,128]{2,1,0:T(8,128)(2,1)S(1)} %pad_maximum_fusion.1.own_ref), channel_id=1, source_target_pairs={{0,8},{8,0},{16,24},{24,16},{32,40},{40,32},{48,56},{56,48},{64,72... | collective-permute-start | bytes 884744 | tf_op jit(solution)/shard_map/ppermute | solution.py:411
  166.1 1.1 copy.55
  167.9 2.3 %unpack.1 = (f32[1024,128]{1,0:T(8,128)}, f32[128,512]{1,0:T(8,128)}, f32[512,128]{1,0:T(8,128)}, f32[256,32]{1,0:T(8,128)}, f32[256,32]{1,0:T(8,128)}) custom-call(s32[1]{0:T(128)} %bitcast.core_ref, bf16[9,128,128]{2,1,0:T(8,128)(2,1)} %copy-done.5, bf16[9,128,128]{2,1,0:T(8,128)(2,1)} %copy-done.10, f32[1]{0:T(128)} %constant.37.clone.1.scale_ref), custom_call_target="tpu_custom_call" | custom-call | tf_op jit(solution)/shard_map/unpack/pallas_call | solution.py:386
  170.2 1.6 copy.56
  171.7 1.6 copy.57
  (67 shorter events, 9.8 us)
Async XLA Ops:
  0.6 11.4 %copy-start = (bf16[256,32]{0,1:T(8,128)(2,1)S(1)}, bf16[256,32]{0,1:T(8,128)(2,1)}, u32[]{:S(2)}) copy-start(bf16[256,32]{0,1:T(8,128)(2,1)} %param.14) | copy-start | bytes 49156
  3.3 8.7 %copy-start.1 = (bf16[128,8,256]{2,1,0:T(8,128)(2,1)S(1)}, bf16[128,8,256]{2,1,0:T(8,128)(2,1)}, u32[]{:S(2)}) copy-start(bf16[128,8,256]{2,1,0:T(8,128)(2,1)} %param.11) | copy-start | bytes 1572868
  3.4 8.7 %copy-start.13 = (f32[256]{0:T(256)S(1)}, f32[256]{0:T(256)}, u32[]{:S(2)}) copy-start(f32[256]{0:T(256)} %param.12) | copy-start | bytes 3076
  5.8 16.8 %all-to-all-start = ((bf16[8,8,32,128]{3,2,1,0:T(8,128)(2,1)}), bf16[8,8,32,128]{3,2,1,0:T(8,128)(2,1)S(1)}, u32[]{:S(2)}, u32[]{:S(2)}) async-start(bf16[8,8,32,128]{3,2,1,0:T(8,128)(2,1)} %broadcast_in_dim.17), calls=%async_computation | async-start | bytes 1048576 | tf_op jit(solution)/shard_map/all_to_all | solution.py:402
  12.0 31.4 %copy-start.7 = (bf16[128,512]{1,0:T(8,128)(2,1)S(1)}, bf16[128,512]{1,0:T(8,128)(2,1)}, u32[]{:S(2)}) copy-start(bf16[128,512]{1,0:T(8,128)(2,1)} %expand_ref.1) | copy-start | bytes 393220
  12.1 32.2 %copy-start.8 = (bf16[512,128]{1,0:T(8,128)(2,1)S(1)}, bf16[512,128]{1,0:T(8,128)(2,1)}, u32[]{:S(2)}) copy-start(bf16[512,128]{1,0:T(8,128)(2,1)} %contract_ref.1) | copy-start | bytes 393220
  12.1 33.0 %copy-start.11 = (bf16[1024,128]{1,0:T(8,128)(2,1)S(1)}, bf16[1024,128]{1,0:T(8,128)(2,1)}, u32[]{:S(2)}) copy-start(bf16[1024,128]{1,0:T(8,128)(2,1)} %param.15) | copy-start | bytes 786436
  12.5 10.1 %collective-permute-start = (bf16[32,8,128]{2,0,1:T(8,128)(2,1)S(1)}, bf16[32,8,128]{2,0,1:T(8,128)(2,1)S(1)}, u32[]{:S(2)}, u32[]{:S(2)}) collective-permute-start(bf16[32,8,128]{2,0,1:T(8,128)(2,1)S(1)} %fusion.7), channel_id=1, source_target_pairs={{0,0},{1,8},{2,16},{3,24},{4,32},{5,40},{6,48},{7,56},{8,64},{9,72... | collective-permute-start | bytes 196616 | tf_op jit(solution)/shard_map/ppermute | solution.py:452
  22.7 23.3 %copy-start.3 = (bf16[8,8,32,128]{3,2,1,0:T(8,128)(2,1)}, bf16[8,8,32,128]{3,2,1,0:T(8,128)(2,1)S(1)}, u32[]{:S(2)}) copy-start(bf16[8,8,32,128]{3,2,1,0:T(8,128)(2,1)S(1)} %all-to-all-done) | copy-start | bytes 1572868
  41.4 4.6 %copy-start.4 = (bf16[8,32,8,128]{3,2,1,0:T(8,128)(2,1)}, bf16[8,32,8,128]{3,2,1,0:T(8,128)(2,1)S(1)}, u32[]{:S(2)}) copy-start(bf16[8,32,8,128]{3,2,1,0:T(8,128)(2,1)S(1)} %all_to_all.30.own_ref) | copy-start | bytes 1572868
  41.4 4.6 %collective-permute-start.1 = (bf16[8,32,8,128]{3,2,1,0:T(8,128)(2,1)S(1)}, bf16[8,32,8,128]{3,2,1,0:T(8,128)(2,1)S(1)}, u32[]{:S(2)}, u32[]{:S(2)}) collective-permute-start(bf16[8,32,8,128]{3,2,1,0:T(8,128)(2,1)S(1)} %all_to_all.30.own_ref), channel_id=1, source_target_pairs={{0,8},{8,0},{16,24},{24,16},{32,40},{40,32},{48,56},{56,48},{64,72... | collective-permute-start | bytes 1572872 | tf_op jit(solution)/shard_map/ppermute | solution.py:411
  45.1 0.9 copy-start.2
  46.0 0.8 copy-start.6
  97.3 2.6 %collective-permute-start.2 = (bf16[8,384,128]{2,1,0:T(8,128)(2,1)}, bf16[8,384,128]{2,1,0:T(8,128)(2,1)S(1)}, u32[]{:S(2)}, u32[]{:S(2)}) collective-permute-start(bf16[8,384,128]{2,1,0:T(8,128)(2,1)} %get-tuple-element.27), channel_id=1, source_target_pairs={{0,8},{8,0},{16,24},{24,16},{32,40},{40,32},{48,56},{56,48},{64,72... | collective-permute-start | bytes 2359304 | tf_op jit(solution)/shard_map/ppermute | solution.py:411
  101.2 17.2 %copy-start.9 = (bf16[2048,128]{1,0:T(8,128)(2,1)S(1)}, bf16[2048,128]{1,0:T(8,128)(2,1)}, u32[]{:S(2)}) copy-start(bf16[2048,128]{1,0:T(8,128)(2,1)} %get-tuple-element.28) | copy-start | bytes 1572868
  119.4 12.4 %all-to-all-start.3 = ((bf16[8,272,128]{2,1,0:T(8,128)(2,1)}), bf16[8,272,128]{2,1,0:T(8,128)(2,1)S(1)}, u32[]{:S(2)}, u32[]{:S(2)}) async-start(bf16[8,272,128]{2,1,0:T(8,128)(2,1)} %pad_maximum_fusion), calls=%async_computation.3 | async-start | bytes 1114112 | tf_op jit(solution)/shard_map/all_to_all | solution.py:402
  122.9 8.3 %collective-permute-start.3 = (bf16[32,8,128]{2,0,1:T(8,128)(2,1)S(1)}, bf16[32,8,128]{2,0,1:T(8,128)(2,1)S(1)}, u32[]{:S(2)}, u32[]{:S(2)}) collective-permute-start(bf16[32,8,128]{2,0,1:T(8,128)(2,1)S(1)} %copy.53), channel_id=1, source_target_pairs={{0,0},{8,1},{16,2},{24,3},{32,4},{40,5},{48,6},{56,7},{64,8},{72,9... | collective-permute-start | bytes 196616 | tf_op jit(solution)/shard_map/ppermute | solution.py:480
  132.3 19.3 %copy-start.12 = (bf16[256,32]{0,1:T(8,128)(2,1)S(1)}, bf16[256,32]{0,1:T(8,128)(2,1)}, u32[]{:S(2)}) copy-start(bf16[256,32]{0,1:T(8,128)(2,1)} %param.13) | copy-start | bytes 49156
  147.5 13.2 %all-to-all-start.5 = ((bf16[8,2,128,128]{3,2,1,0:T(8,128)(2,1)}), bf16[8,2,128,128]{3,2,1,0:T(8,128)(2,1)S(1)}, u32[]{:S(2)}, u32[]{:S(2)}) async-start(bf16[8,2,128,128]{3,2,1,0:T(8,128)(2,1)} %broadcast_in_dim.22), calls=%async_computation.5 | async-start | bytes 1048576 | tf_op jit(solution)/shard_map/all_to_all | solution.py:402
  160.8 6.4 %copy-start.5 = (bf16[9,128,128]{2,1,0:T(8,128)(2,1)}, bf16[9,128,128]{2,1,0:T(8,128)(2,1)S(1)}, u32[]{:S(2)}) copy-start(bf16[9,128,128]{2,1,0:T(8,128)(2,1)S(1)} %pad_maximum_fusion.1.own_ref) | copy-start | bytes 884740
  160.8 6.4 %collective-permute-start.4 = (bf16[9,128,128]{2,1,0:T(8,128)(2,1)S(1)}, bf16[9,128,128]{2,1,0:T(8,128)(2,1)S(1)}, u32[]{:S(2)}, u32[]{:S(2)}) collective-permute-start(bf16[9,128,128]{2,1,0:T(8,128)(2,1)S(1)} %pad_maximum_fusion.1.own_ref), channel_id=1, source_target_pairs={{0,8},{8,0},{16,24},{24,16},{32,40},{40,32},{48,56},{56,48},{64,72... | collective-permute-start | bytes 884744 | tf_op jit(solution)/shard_map/ppermute | solution.py:411
  167.2 0.7 copy-start.10

commit v3 on v2

--- a/solution.py
+++ b/solution.py
@@ -21,24 +21,6 @@
 
 def matmul_nt(a, b):
     return lax.dot_general(a, b, (((1,), (1,)), ((), ())), preferred_element_type=F32)
-
-
-def standardize_features(values, gain_vec):
-    average = jnp.mean(values, axis=-1, keepdims=True)
-    centred = values - average
-    variance = jnp.mean(centred * centred, axis=-1, keepdims=True)
-    inv_scale = lax.rsqrt(variance + EPSILON)
-    vhat_values = centred * inv_scale
-    return (vhat_values * gain_vec, vhat_values, inv_scale)
-
-
-def standardize_reverse_mode(incoming, vhat_values, inv_scale, gain_vec):
-    scaled = incoming * gain_vec
-    return inv_scale * (
-        scaled
-        - jnp.mean(scaled, axis=-1, keepdims=True)
-        - vhat_values * jnp.mean(scaled * vhat_values, axis=-1, keepdims=True)
-    )
 
 
 def pair_kernel(
@@ -109,7 +91,7 @@
             acc_left[...] += part
         else:
             total = (acc_left[...] + part) * (1.0 / seqs)
-            d_left_ref[pl.ds(pl.multiple_of(b * rows, rows), rows), :] = total.astype(BF16)
+            d_left_ref[b, :rows, :] = total.astype(BF16)
 
     @pl.when(step == 0)
     def _():
@@ -264,7 +246,8 @@
             other_out_ref[m, base:, :] = jnp.where(first, odd, even).astype(BF16)
 
 
-def pair_stage(core, left, own, other, pair, cot, proj, expand, contract, offset, gain):
+def pair_stage(core, left, own, other, pair, cot, weights, offset, gain, devices):
+    by_e, by_e_t, expand, expand_t, contract, contract_t = weights
     each = own.shape[2]
     rows, lanes, width = pair.shape
     seqs = left.shape[1]
@@ -272,12 +255,10 @@
     wide = channels * lanes
     hidden = expand.shape[1]
     block = 8
-    by_e = (
-        proj.reshape(channels, channels, width).transpose(1, 0, 2).reshape(channels * channels, width)
-    )
     whole = lambda shape: pl.BlockSpec(shape, lambda b: (0,) * len(shape))
-    weights = channels * channels + 2 * hidden
-    parts = (own.shape[0], channels * each + weights // (2 * own.shape[0]), width)
+    grads = channels * channels + 2 * hidden
+    d_left = (rows // block, block * channels + grads // devices, seqs)
+    parts = (own.shape[0], channels * each + grads // (2 * own.shape[0]), width)
     tiles = pl.BlockSpec((block, lanes, width), lambda b: (b, 0, 0))
     flat = whole((rows * channels, seqs))
     return pl.pallas_call(
@@ -302,14 +283,14 @@
         out_specs=[
             tiles,
             tiles,
-            flat,
+            whole(d_left),
             whole(parts),
             whole(parts),
         ],
         out_shape=[
             jax.ShapeDtypeStruct((rows, lanes, width), BF16),
             jax.ShapeDtypeStruct((rows, lanes, width), BF16),
-            jax.ShapeDtypeStruct((rows * channels, seqs), BF16),
+            jax.ShapeDtypeStruct(d_left, BF16),
             jax.ShapeDtypeStruct(parts, BF16),
             jax.ShapeDtypeStruct(parts, BF16),
         ],
@@ -338,12 +319,7 @@
         other,
         pair,
         cot,
-        by_e,
-        by_e.T,
-        expand,
-        expand.T,
-        contract,
-        contract.T,
+        *weights,
         offset.astype(F32)[None, :],
         gain.astype(F32)[None, :],
     )
@@ -372,12 +348,12 @@
     for k in range(contract_ref.shape[0] // size):
         contract_ref[k * size : (k + 1) * size, :] = chunk(at)
         at += 1
-    factors = ((own_ref[0].astype(F32) + other_ref[0].astype(F32)) * scale).T
-    channels = left_ref.shape[1]
-    for h in range(left_ref.shape[0] // size):
-        rows = slice(h * size, (h + 1) * size)
-        left_ref[rows, :] = factors[:, 2 * h * channels : (2 * h + 1) * channels]
-        right_ref[rows, :] = factors[:, (2 * h + 1) * channels : (2 * h + 2) * channels]
+    factors = (own_ref[0].astype(F32) + other_ref[0].astype(F32)) * scale
+    channels = left_ref.shape[0]
+    for h in range(left_ref.shape[1] // size):
+        at = slice(h * size, (h + 1) * size)
+        left_ref[:, at] = factors[2 * h * channels : (2 * h + 1) * channels]
+        right_ref[:, at] = factors[(2 * h + 1) * channels : (2 * h + 2) * channels]
 
 
 def unpack(core, own, other, scale, shapes):
@@ -388,8 +364,121 @@
         in_specs=[smem, vmem, vmem, smem],
         out_specs=[vmem] * len(shapes),
         out_shape=[jax.ShapeDtypeStruct(shape, F32) for shape in shapes],
+        compiler_params=pltpu.CompilerParams(vmem_limit_bytes=16 * 1024 * 1024),
         name="unpack",
     )(core, own, other, jnp.full((1,), scale, F32))
+
+
+def project_kernel(x_ref, gain_ref, first_ref, second_ref, left_ref, right_ref, normed_ref, *halves):
+    seqs, residues, features = x_ref.shape
+    channels = right_ref.shape[0]
+    x = x_ref[...].astype(F32)
+    centred = x - jnp.mean(x, axis=-1, keepdims=True)
+    variance = jnp.mean(centred * centred, axis=-1, keepdims=True)
+    vhat = centred * lax.rsqrt(variance + EPSILON)
+    factors = jnp.concatenate([first_ref[...], second_ref[...]], axis=0)
+    lanes = halves[0].shape[1]
+    rows = (vhat * gain_ref[...][None]).reshape(seqs * residues, features)
+    for h, scr in enumerate(halves):
+        scr[...] = rows[:, h * lanes : (h + 1) * lanes]
+    for r in range(residues):
+        normed = jnp.concatenate(
+            [scr[pl.ds(r, seqs, stride=residues), :] for scr in halves], axis=1
+        ).astype(BF16)
+        normed_ref[r] = normed
+        both = matmul_nt(factors, normed).astype(BF16)
+        left = both[:channels] * (1.0 / seqs)
+        for k in range(left_ref.shape[0]):
+            left_ref[k, r] = left
+        right_ref[:, r, :] = both[channels:]
+
+
+def project(x, gain, first, second, copies):
+    seqs, residues, features = x.shape
+    channels = first.shape[0]
+    vmem = pl.BlockSpec(memory_space=pltpu.VMEM)
+    return pl.pallas_call(
+        project_kernel,
+        in_specs=[vmem] * 4,
+        out_specs=[vmem] * 3,
+        out_shape=[
+            jax.ShapeDtypeStruct((copies, residues, channels, seqs), BF16),
+            jax.ShapeDtypeStruct((channels, residues, seqs), BF16),
+            jax.ShapeDtypeStruct((residues, seqs, features), BF16),
+        ],
+        scratch_shapes=[pltpu.VMEM((seqs * residues, 128), F32)] * (features // 128),
+        name="project",
+    )(x, gain[None, :], first, second)
+
+
+def factor_grad_kernel(normed_ref, left_ref, right_ref, weights_ref, out_ref):
+    residues, seqs, features = normed_ref.shape
+    total = 0.0
+    for r in range(residues):
+        both = jnp.concatenate([left_ref[r], right_ref[:, r, :]], axis=0)
+        total = total + matmul(both, normed_ref[r])
+    size = out_ref.shape[2]
+    parts = [total[:, k : k + size].astype(BF16) for k in range(0, features, size)]
+    rows = jnp.concatenate(parts + [weights_ref[...]], axis=0)
+    for k in range(out_ref.shape[0]):
+        out_ref[k] = rows
+
+
+def factor_grad(normed, left, right, weights, copies):
+    vmem = pl.BlockSpec(memory_space=pltpu.VMEM)
+    lanes = weights.shape[1]
+    rows = 2 * right.shape[0] * (normed.shape[2] // lanes) + weights.shape[0]
+    return pl.pallas_call(
+        factor_grad_kernel,
+        in_specs=[vmem] * 4,
+        out_specs=vmem,
+        out_shape=jax.ShapeDtypeStruct((copies, rows, lanes), BF16),
+        compiler_params=pltpu.CompilerParams(vmem_limit_bytes=16 * 1024 * 1024),
+        name="factor_grad",
+    )(normed, left, right, weights)
+
+
+def align_grad_kernel(x_ref, gain_ref, first_ref, second_ref, left_ref, right_ref, out_ref, *halves):
+    seqs, residues, features = x_ref.shape
+    lanes = halves[0].shape[1]
+    factors = jnp.concatenate([first_ref[...], second_ref[...]], axis=0)
+    for r in range(residues):
+        both = jnp.concatenate([left_ref[r], right_ref[:, r, :]], axis=0)
+        grad = lax.dot_general(
+            both, factors, (((0,), (0,)), ((), ())), preferred_element_type=F32
+        )
+        for h, scr in enumerate(halves):
+            scr[pl.ds(r, seqs, stride=residues), :] = grad[:, h * lanes : (h + 1) * lanes]
+    x = x_ref[...].astype(F32)
+    centred = x - jnp.mean(x, axis=-1, keepdims=True)
+    variance = jnp.mean(centred * centred, axis=-1, keepdims=True)
+    inv = lax.rsqrt(variance + EPSILON)
+    vhat = centred * inv
+    grad = jnp.concatenate([scr[...] for scr in halves], axis=1)
+    scaled = grad.reshape(seqs, residues, features) * gain_ref[...][None]
+    grad = inv * (
+        scaled
+        - jnp.mean(scaled, axis=-1, keepdims=True)
+        - vhat * jnp.mean(scaled * vhat, axis=-1, keepdims=True)
+    )
+    out_ref[...] = grad.astype(BF16)
+
+
+def align_grad(x, gain, first, second, left, right):
+    seqs, residues, features = x.shape
+    vmem = pl.BlockSpec(memory_space=pltpu.VMEM)
+    return pl.pallas_call(
+        align_grad_kernel,
+        in_specs=[vmem] * 6,
+        out_specs=vmem,
+        out_shape=jax.ShapeDtypeStruct(x.shape, BF16),
+        scratch_shapes=[pltpu.VMEM((seqs * residues, 128), F32)] * (features // 128),
+        cost_estimate=pl.CostEstimate(
+            flops=300 * x.size, transcendentals=seqs * residues, bytes_accessed=5 * x.size
+        ),
+        compiler_params=pltpu.CompilerParams(vmem_limit_bytes=16 * 1024 * 1024),
+        name="align_grad",
+    )(x, gain[None, :], first, second, left, right)
 
 
 def parity_groups():
@@ -438,20 +527,20 @@
     row_count, col_count, pair_width = couple_tensor.shape
     rows, cols = lax.axis_size("row"), lax.axis_size("col")
     amino_number = row_count * rows
-    normed_full, msa_hat, msa_inv = standardize_features(
-        alignment_tensor.astype(F32), alignment_scaling_vector
-    )
-    normed = normed_full.astype(BF16)
-    left_local = jnp.einsum(
-        "srm,mc->rcs", normed, first_factor_matrix, preferred_element_type=F32
-    ).astype(BF16)
-    right_local = jnp.einsum(
-        "srm,me->ers", normed, second_factor_matrix, preferred_element_type=F32
-    ).astype(BF16)
+    gain = alignment_scaling_vector.astype(F32)
+    first_t, second_t = first_factor_matrix.T, second_factor_matrix.T
+    left_copies, right_local, normed = project(alignment_tensor, gain, first_t, second_t, cols)
+    by_e = (
+        final_mapping_matrix.reshape(channels, channels, pair_width)
+        .transpose(1, 0, 2)
+        .reshape(channels * channels, pair_width)
+    )
+    turned = (by_e, by_e.T, feedforward_expand_matrix.T, feedforward_contract_matrix.T)
     there, back = column_pairs(rows, cols)
     right_moved = lax.ppermute(right_local, BOTH, there)
-    left_rows = spread(left_local * (1.0 / aligned_number), "col")
-    right_moved, left_rows = lax.optimization_barrier((right_moved, left_rows))
+    left_rows = exchange(left_copies, "col")
+    right_moved, left_rows, turned = lax.optimization_barrier((right_moved, left_rows, turned))
+    by_e, by_e_t, expand_t, contract_t = turned
     own = spread(right_moved, "row")
     other = from_partner(own)
     core = (lax.axis_index("row") % 2).astype(jnp.int32)[None]
@@ -462,19 +551,18 @@
         other,
         couple_tensor,
         upstream_sensitivity,
-        final_mapping_matrix,
-        feedforward_expand_matrix,
-        feedforward_contract_matrix,
+        (by_e, by_e_t, feedforward_expand_matrix, expand_t, feedforward_contract_matrix, contract_t),
         final_offset_vector,
         feedforward_scaling_vector,
+        rows * cols,
     )
     lanes = pair_width
     mine = (mine.astype(F32) + from_partner(theirs).astype(F32)).astype(BF16)
     mine = summed(exchange(mine, "row"))
     size = channels * shard_extent
     d_right = mine[:size].reshape(channels, shard_extent, aligned_number)
-    with_left = jnp.concatenate(
-        [d_left.reshape(cols, size, lanes), mine[size:].reshape(cols, -1, lanes)], axis=1
+    with_left = lax.dynamic_update_slice(
+        d_left, mine[size:].reshape(cols, -1, lanes), (0, size, 0)
     )
     d_right, with_left = lax.optimization_barrier((d_right, with_left))
     d_right = lax.ppermute(d_right, BOTH, back)
@@ -482,30 +570,16 @@
     d_left = with_left[:size].reshape(shard_extent, channels, aligned_number)
     weights = with_left[size:]
 
-    left_weight = jnp.einsum("srm,rcs->cm", normed, d_left, preferred_element_type=F32)
-    right_weight = jnp.einsum("srm,ers->em", normed, d_right, preferred_element_type=F32)
-    d_normed = jnp.einsum("rcs,mc->srm", d_left, first_factor_matrix, preferred_element_type=F32)
-    d_normed = d_normed + jnp.einsum(
-        "ers,me->srm", d_right, second_factor_matrix, preferred_element_type=F32
-    )
-    alignment_sensitivity = standardize_reverse_mode(
-        d_normed, msa_hat, msa_inv, alignment_scaling_vector
-    ).astype(BF16)
-
-    factors = jnp.concatenate(
-        [
-            weight[:, k : k + lanes].astype(BF16)
-            for k in range(0, features, lanes)
-            for weight in (left_weight, right_weight)
-        ],
-        axis=0,
-    )
-    count = factors.shape[0]
-    gathered = spread(jnp.concatenate([factors, weights], axis=0), "col")
+    gathered = exchange(factor_grad(normed, d_left, d_right, weights, cols), "col")
+    count = gathered.shape[1] - weights.shape[0]
     factors = summed(gathered[:, :count])
     weights = gathered[:, count:].reshape(-1, lanes)
     gathered = spread(jnp.stack([factors, weights], axis=0), "row")
+    alignment_sensitivity = align_grad(
+        alignment_tensor, gain, first_t, second_t, d_left, d_right
+    )
     half = jnp.concatenate([summed(gathered[:, 0])[None], gathered[:, 1]], axis=0)
+    half, alignment_sensitivity = lax.optimization_barrier((half, alignment_sensitivity))
     outs = unpack(
         core,
         half,
@@ -515,11 +589,11 @@
             final_mapping_matrix.shape,
             feedforward_expand_matrix.shape,
             feedforward_contract_matrix.shape,
-            first_factor_matrix.shape,
-            second_factor_matrix.shape,
+            first_factor_matrix.shape[::-1],
+            second_factor_matrix.shape[::-1],
         ),
     )
-    return (result, grad, alignment_sensitivity, *outs)
+    return (result, grad, alignment_sensitivity, *outs[:3], outs[3].T, outs[4].T)
 
 
 def solution(mesh):

time: 174 us -> 164 us (0.943)
  other arithmetic: 5.9 us -> 1.64 us
  matrix products: 4.21 us -> 0 us
  Pallas kernels: 52.8 us -> 56.5 us
  local copies, waits for them, and re-layouts: 10.3 us -> 6.73 us
    pallas_call x0 -> x3, Pallas kernels: none -> 4.97 us  [the longest x1 2.9 us: project(): pl.pallas_call(project_kernel, in_specs=[vmem] * 4, out_specs=[vmem] * 3,...]
    dot_general x6 -> x0, matrix products: 4.21 us -> none  [the longest x1 1.56 us: on_device(): jnp.einsum('srm,mc->rcs', normed, first_factor_matrix, preferred_element_...]
    ppermute x1, waiting for transfers between devices: 4.04 us -> 0.29 us  [on_device(): right_moved = lax.ppermute(right_local, BOTH, there)]
    all_to_all x3, waiting for transfers between devices: 7.77 us -> 11.3 us  [exchange(): return lax.all_to_all(x, axis, 0, 0, tiled=True, axis_index_groups=groups)]
    ppermute x1, waiting for transfers between devices: 3.46 us -> 0.01 us  [on_device(): d_right = lax.ppermute(d_right, BOTH, back)]
    unnamed x37 -> x22, local copies, waits for them, and re-layouts: 7.4 us -> 4.17 us
    reduce_sum x2 -> x0, other arithmetic: 2.67 us -> none  [the longest x1 1.42 us: standardize_features(): variance = jnp.mean(centred * centred, axis=-1, keepdims=True)]
    ppermute x3, waiting for transfers between devices: 2.44 us -> 4.87 us  [from_partner(): lax.ppermute(x, 'row', [(k, k ^ 1) for k in range(lax.axis_size('row'))])]
  transfers between devices with their start and end apart: 8 -> 8, of which waited for: 4 -> 6; matrix products, arithmetic and copies ran while one was open for 4% -> 3% of each run, Pallas kernels for 0% -> 1%
where the time goes in v3:
time: 164 us; the launch traced here: 163 us
  Pallas kernels  56.5 us (34%)
  blocking collectives  49.4 us (30%)
  starting transfers between devices  31.7 us (19%)
  waiting for transfers between devices  16.5 us (10%)
  local copies, waits for them, and re-layouts  6.73 us (4%)
    pallas_call x1, Pallas kernels, pair_stage(): pl.pallas_call(pair_kernel, grid=(rows // block,), in_specs=[pl.BlockSpec...  50.6 us
    all_to_all x3, blocking collectives, exchange(): return lax.all_to_all(x, axis, 0, 0, tiled=True, axis_index_groups=groups)  49.4 us
    all_to_all x3, starting transfers between devices, exchange(): return lax.all_to_all(x, axis, 0, 0, tiled=True, axis_index_groups=groups)  13.8 us
    all_to_all x3, waiting for transfers between devices, exchange(): return lax.all_to_all(x, axis, 0, 0, tiled=True, axis_index_groups=groups)  11.3 us
    ppermute x3, starting transfers between devices, from_partner(): lax.ppermute(x, 'row', [(k, k ^ 1) for k in range(lax.axis_size('row'))])  7.11 us
    ppermute x1, starting transfers between devices, on_device(): right_moved = lax.ppermute(right_local, BOTH, there)  6.04 us
    ppermute x3, waiting for transfers between devices, from_partner(): lax.ppermute(x, 'row', [(k, k ^ 1) for k in range(lax.axis_size('row'))])  4.87 us
    ppermute x1, starting transfers between devices, on_device(): d_right = lax.ppermute(d_right, BOTH, back)  4.74 us
  transfers between devices with their start and end apart: 8, of which 6 were waited for; matrix products, arithmetic and copies ran while one was open for 3% of the time, Pallas kernels for 1%

profile of v3, /device:TPU:1, one launch (start us, length us, event | category | flops | bytes accessed | tf_op | source)
XLA Modules:
  0.0 163.2 jit_solution(1663125456754835794)
XLA Ops:
  0.6 2.9 %project.1 = (bf16[8,8,32,128]{3,2,1,0:T(8,128)(2,1)}, bf16[32,8,128]{2,1,0:T(8,128)(2,1)}, bf16[8,128,256]{2,1,0:T(8,128)(2,1)}) custom-call(bf16[128,8,256]{2,1,0:T(8,128)(2,1)} %x_ref.3, f32[1,256]{1,0:T(1,128)} %bitcast.33, bf16[32,256]{1,0:T(8,128)(2,1)} %bitcast.29, bf16[32,256]{1,0:T(8,128)(2,1)} %bitcast.31), custom_call_target="tpu_custom_call" | custom-call | tf_op jit(solution)/shard_map/project/pallas_call | solution.py:400
  3.5 6.2 %all-to-all-start = ((bf16[8,8,32,128]{3,2,1,0:T(8,128)(2,1)}), bf16[8,8,32,128]{3,2,1,0:T(8,128)(2,1)S(1)}, u32[]{:S(2)}, u32[]{:S(2)}) async-start(bf16[8,8,32,128]{3,2,1,0:T(8,128)(2,1)} %get-tuple-element.32), calls=%async_computation | async-start | bytes 1048576 | tf_op jit(solution)/shard_map/all_to_all | solution.py:491
  9.7 6.0 %collective-permute-start = (bf16[32,8,128]{2,1,0:T(8,128)(2,1)}, bf16[32,8,128]{2,1,0:T(8,128)(2,1)S(1)}, u32[]{:S(2)}, u32[]{:S(2)}) collective-permute-start(bf16[32,8,128]{2,1,0:T(8,128)(2,1)} %get-tuple-element.31), channel_id=1, source_target_pairs={{0,0},{1,8},{2,16},{3,24},{4,32},{5,40},{6,48},{7,56},{8,64},{9,72... | collective-permute-start | bytes 196616 | tf_op jit(solution)/shard_map/ppermute | solution.py:540
  15.8 1.7 %copy.32 = bf16[128,512]{0,1:T(8,128)(2,1)} copy(bf16[128,512]{1,0:T(8,128)(2,1)} %expand_ref.1) | data formatting | bytes 262144 | tf_op args[8]
  17.4 1.7 %copy.33 = bf16[512,128]{0,1:T(8,128)(2,1)} copy(bf16[512,128]{1,0:T(8,128)(2,1)} %contract_ref.1) | data formatting | bytes 262144 | tf_op args[9]
  19.2 0.9 copy.31
  20.4 18.5 %all_to_all.30.own_ref = bf16[8,32,8,128]{3,2,1,0:T(8,128)(2,1)S(1)} all-to-all(bf16[8,32,8,128]{3,2,1,0:T(8,128)(2,1)S(1)} %broadcast_in_dim.30), channel_id=1, replica_groups={{0,16,32,48,64,80,96,112},{8,24,40,56,72,88,104,120},{1,17,33,49,65,81,..., dimensions={0} | all-to-all | bytes 1048576 | tf_op jit(solution)/shard_map/all_to_all | solution.py:491
  39.0 2.1 %collective-permute-start.1 = (bf16[8,32,8,128]{3,2,1,0:T(8,128)(2,1)S(1)}, bf16[8,32,8,128]{3,2,1,0:T(8,128)(2,1)S(1)}, u32[]{:S(2)}, u32[]{:S(2)}) collective-permute-start(bf16[8,32,8,128]{3,2,1,0:T(8,128)(2,1)S(1)} %all_to_all.30.own_ref), channel_id=1, source_target_pairs={{0,8},{8,0},{16,24},{24,16},{32,40},{40,32},{48,56},{56,48},{64,72... | collective-permute-start | bytes 1572872 | tf_op jit(solution)/shard_map/ppermute | solution.py:500
  41.1 1.5 collective-permute-done.1.other_ref
  43.4 50.6 %pair_stage.1 = (bf16[64,128,128]{2,1,0:T(8,128)(2,1)}, bf16[64,128,128]{2,1,0:T(8,128)(2,1)}, bf16[8,272,128]{2,1,0:T(8,128)(2,1)}, bf16[8,384,128]{2,1,0:T(8,128)(2,1)}, bf16[8,384,128]{2,1,0:T(8,128)(2,1)}) custom-call(s32[1]{0:T(128)} %bitcast.core_ref, bf16[2048,128]{1,0:T(8,128)(2,1)} %bitcast.37, bf16[8,32,8,128]{3,2,1,0:T(8,128)(2,1)} %copy-done.7, ...), custom_call_target="tpu_custom_call" | custom-call | tf_op jit(solution)/shard_map/pair_stage/pallas_call | solution.py:264
  94.4 2.1 %collective-permute-done.2 = bf16[8,384,128]{2,1,0:T(8,128)(2,1)S(1)} collective-permute-done((bf16[8,384,128]{2,1,0:T(8,128)(2,1)}, bf16[8,384,128]{2,1,0:T(8,128)(2,1)S(1)}, u32[]{:S(2)}, u32[]{:S(2)}) %collective-permute-start.2) | collective-permute-done | bytes 786464 | tf_op jit(solution)/shard_map/ppermute | solution.py:500
  96.6 1.3 add_convert_fusion
  97.9 17.1 %all_to_all.31 = bf16[8,384,128]{2,1,0:T(8,128)(2,1)S(1)} all-to-all(bf16[8,384,128]{2,1,0:T(8,128)(2,1)S(1)} %add_convert_fusion), channel_id=1, replica_groups={{0,16,32,48,64,80,96,112},{8,24,40,56,72,88,104,120},{1,17,33,49,65,81,..., dimensions={0} | all-to-all | bytes 1572864 | tf_op jit(solution)/shard_map/all_to_all | solution.py:491
  115.8 3.6 %all-to-all-start.3 = ((bf16[8,272,128]{2,1,0:T(8,128)(2,1)}), bf16[8,272,128]{2,1,0:T(8,128)(2,1)S(1)}, u32[]{:S(2)}, u32[]{:S(2)}) async-start(bf16[8,272,128]{2,1,0:T(8,128)(2,1)} %constant_dynamic-update-slice_fusion), calls=%async_computation.3 | async-start | bytes 1114112 | tf_op jit(solution)/shard_map/all_to_all | solution.py:491
  119.4 4.7 %collective-permute-start.3 = (bf16[32,8,128]{2,1,0:T(8,128)(2,1)S(1)}, bf16[32,8,128]{2,1,0:T(8,128)(2,1)S(1)}, u32[]{:S(2)}, u32[]{:S(2)}) collective-permute-start(bf16[32,8,128]{2,1,0:T(8,128)(2,1)S(1)} %slice_bitcast_fusion.1), channel_id=1, source_target_pairs={{0,0},{8,1},{16,2},{24,3},{32,4},{40,5},{48,6},{56,7},{64,8},{72,9... | collective-permute-start | bytes 196616 | tf_op jit(solution)/shard_map/ppermute | solution.py:568
  124.2 4.1 %all-to-all-done.3 = bf16[8,272,128]{2,1,0:T(8,128)(2,1)S(1)} async-done(((bf16[8,272,128]{2,1,0:T(8,128)(2,1)}), bf16[8,272,128]{2,1,0:T(8,128)(2,1)S(1)}, u32[]{:S(2)}, u32[]{:S(2)}) %all-to-all-start.3) | async-done | bytes 557088 | tf_op jit(solution)/shard_map/all_to_all | solution.py:491
  128.6 13.7 %all_to_all.32 = bf16[8,144,128]{2,1,0:T(8,128)(2,1)S(1)} all-to-all(bf16[8,144,128]{2,1,0:T(8,128)(2,1)S(1)} %factor_grad.1), channel_id=1, replica_groups=mesh['row'=16,'col'=8] {'col'}, dimensions={0} | all-to-all | bytes 589824 | tf_op jit(solution)/shard_map/all_to_all | solution.py:491
  142.4 0.9 broadcast_in_dim.33
  143.3 4.0 %all-to-all-start.5 = ((bf16[8,2,128,128]{3,2,1,0:T(8,128)(2,1)}), bf16[8,2,128,128]{3,2,1,0:T(8,128)(2,1)S(1)}, u32[]{:S(2)}, u32[]{:S(2)}) async-start(bf16[8,2,128,128]{3,2,1,0:T(8,128)(2,1)} %broadcast_in_dim.33), calls=%async_computation.5 | async-start | bytes 1048576 | tf_op jit(solution)/shard_map/all_to_all | solution.py:491
  147.3 1.8 %align_grad.1 = bf16[128,8,256]{2,1,0:T(8,128)(2,1)} custom-call(bf16[128,8,256]{2,1,0:T(8,128)(2,1)S(1)} %copy-done, f32[1,256]{1,0:T(1,128)S(1)} %bitcast.34, bf16[32,256]{1,0:T(8,128)(2,1)S(1)} %bitcast.30, bf16[32,256]{1,0:T(8,128)(2,1)S(1)} %bitcast.32, bf16[8,32,128]{2,1,0:T(8,128)(2,1)S(1)} %bitcast.28, ...), custom_call_target="tpu_custom_call" | custom-call | flops 78643200 | bytes 1310720 | tf_op jit(solution)/shard_map/align_grad/pallas_call | solution.py:470
  149.1 7.2 %all-to-all-done.5 = bf16[8,2,128,128]{3,2,1,0:T(8,128)(2,1)S(1)} async-done(((bf16[8,2,128,128]{3,2,1,0:T(8,128)(2,1)}), bf16[8,2,128,128]{3,2,1,0:T(8,128)(2,1)S(1)}, u32[]{:S(2)}, u32[]{:S(2)}) %all-to-all-start.5) | async-done | bytes 524320 | tf_op jit(solution)/shard_map/all_to_all | solution.py:491
  156.4 4.6 %collective-permute-start.4 = (bf16[9,128,128]{2,1,0:T(8,128)(2,1)S(1)}, bf16[9,128,128]{2,1,0:T(8,128)(2,1)S(1)}, u32[]{:S(2)}, u32[]{:S(2)}) collective-permute-start(bf16[9,128,128]{2,1,0:T(8,128)(2,1)S(1)} %pad_maximum_fusion.own_ref), channel_id=1, source_target_pairs={{0,8},{8,0},{16,24},{24,16},{32,40},{40,32},{48,56},{56,48},{64,72... | collective-permute-start | bytes 884744 | tf_op jit(solution)/shard_map/ppermute | solution.py:500
  161.0 1.2 collective-permute-done.4.other_ref
  162.2 1.0 unpack.1
  (39 shorter events, 3.0 us)
Async XLA Ops:
  0.6 18.5 %copy-start.9 = (bf16[1024,128]{1,0:T(8,128)(2,1)S(1)}, bf16[1024,128]{1,0:T(8,128)(2,1)}, u32[]{:S(2)}) copy-start(bf16[1024,128]{1,0:T(8,128)(2,1)} %param.15) | copy-start | bytes 786436
  3.5 16.8 %all-to-all-start = ((bf16[8,8,32,128]{3,2,1,0:T(8,128)(2,1)}), bf16[8,8,32,128]{3,2,1,0:T(8,128)(2,1)S(1)}, u32[]{:S(2)}, u32[]{:S(2)}) async-start(bf16[8,8,32,128]{3,2,1,0:T(8,128)(2,1)} %get-tuple-element.32), calls=%async_computation | async-start | bytes 1048576 | tf_op jit(solution)/shard_map/all_to_all | solution.py:491
  9.7 10.6 %collective-permute-start = (bf16[32,8,128]{2,1,0:T(8,128)(2,1)}, bf16[32,8,128]{2,1,0:T(8,128)(2,1)S(1)}, u32[]{:S(2)}, u32[]{:S(2)}) collective-permute-start(bf16[32,8,128]{2,1,0:T(8,128)(2,1)} %get-tuple-element.31), channel_id=1, source_target_pairs={{0,0},{1,8},{2,16},{3,24},{4,32},{5,40},{6,48},{7,56},{8,64},{9,72... | collective-permute-start | bytes 196616 | tf_op jit(solution)/shard_map/ppermute | solution.py:540
  19.2 23.4 %copy-start.5 = (bf16[32,32,128]{2,1,0:T(8,128)(2,1)}, bf16[32,32,128]{2,1,0:T(8,128)(2,1)S(1)}, u32[]{:S(2)}) copy-start(bf16[32,32,128]{2,1,0:T(8,128)(2,1)S(1)} %copy.30) | copy-start | bytes 786436
  20.4 22.3 %copy-start.6 = (bf16[8,8,32,128]{3,2,1,0:T(8,128)(2,1)}, bf16[8,8,32,128]{3,2,1,0:T(8,128)(2,1)S(1)}, u32[]{:S(2)}) copy-start(bf16[8,8,32,128]{3,2,1,0:T(8,128)(2,1)S(1)} %all-to-all-done) | copy-start | bytes 1572868
  39.0 3.6 %copy-start.7 = (bf16[8,32,8,128]{3,2,1,0:T(8,128)(2,1)}, bf16[8,32,8,128]{3,2,1,0:T(8,128)(2,1)S(1)}, u32[]{:S(2)}) copy-start(bf16[8,32,8,128]{3,2,1,0:T(8,128)(2,1)S(1)} %all_to_all.30.own_ref) | copy-start | bytes 1572868
  39.0 3.6 %collective-permute-start.1 = (bf16[8,32,8,128]{3,2,1,0:T(8,128)(2,1)S(1)}, bf16[8,32,8,128]{3,2,1,0:T(8,128)(2,1)S(1)}, u32[]{:S(2)}, u32[]{:S(2)}) collective-permute-start(bf16[8,32,8,128]{3,2,1,0:T(8,128)(2,1)S(1)} %all_to_all.30.own_ref), channel_id=1, source_target_pairs={{0,8},{8,0},{16,24},{24,16},{32,40},{40,32},{48,56},{56,48},{64,72... | collective-permute-start | bytes 1572872 | tf_op jit(solution)/shard_map/ppermute | solution.py:500
  42.6 0.8 copy-start.8
  94.0 2.6 %collective-permute-start.2 = (bf16[8,384,128]{2,1,0:T(8,128)(2,1)}, bf16[8,384,128]{2,1,0:T(8,128)(2,1)S(1)}, u32[]{:S(2)}, u32[]{:S(2)}) collective-permute-start(bf16[8,384,128]{2,1,0:T(8,128)(2,1)} %get-tuple-element.43), channel_id=1, source_target_pairs={{0,8},{8,0},{16,24},{24,16},{32,40},{40,32},{48,56},{56,48},{64,72... | collective-permute-start | bytes 2359304 | tf_op jit(solution)/shard_map/ppermute | solution.py:500
  97.9 30.4 %copy-start.1 = (bf16[8,128,256]{2,1,0:T(8,128)(2,1)S(1)}, bf16[8,128,256]{2,1,0:T(8,128)(2,1)}, u32[]{:S(2)}) copy-start(bf16[8,128,256]{2,1,0:T(8,128)(2,1)} %get-tuple-element.41.normed_ref) | copy-start | bytes 1572868
  115.8 12.5 %all-to-all-start.3 = ((bf16[8,272,128]{2,1,0:T(8,128)(2,1)}), bf16[8,272,128]{2,1,0:T(8,128)(2,1)S(1)}, u32[]{:S(2)}, u32[]{:S(2)}) async-start(bf16[8,272,128]{2,1,0:T(8,128)(2,1)} %constant_dynamic-update-slice_fusion), calls=%async_computation.3 | async-start | bytes 1114112 | tf_op jit(solution)/shard_map/all_to_all | solution.py:491
  119.4 27.9 %copy-start = (bf16[128,8,256]{2,1,0:T(8,128)(2,1)S(1)}, bf16[128,8,256]{2,1,0:T(8,128)(2,1)}, u32[]{:S(2)}) copy-start(bf16[128,8,256]{2,1,0:T(8,128)(2,1)} %x_ref.3) | copy-start | bytes 1572868
  119.4 27.9 %copy-start.2 = (bf16[256,32]{0,1:T(8,128)(2,1)S(1)}, bf16[256,32]{0,1:T(8,128)(2,1)}, u32[]{:S(2)}) copy-start(bf16[256,32]{0,1:T(8,128)(2,1)} %param.13) | copy-start | bytes 49156
  119.4 27.9 %copy-start.3 = (bf16[256,32]{0,1:T(8,128)(2,1)S(1)}, bf16[256,32]{0,1:T(8,128)(2,1)}, u32[]{:S(2)}) copy-start(bf16[256,32]{0,1:T(8,128)(2,1)} %param.14) | copy-start | bytes 49156
  119.4 27.9 %copy-start.4 = (f32[256]{0:T(256)S(1)}, f32[256]{0:T(256)}, u32[]{:S(2)}) copy-start(f32[256]{0:T(256)} %param.12) | copy-start | bytes 3076
  119.4 8.9 %collective-permute-start.3 = (bf16[32,8,128]{2,1,0:T(8,128)(2,1)S(1)}, bf16[32,8,128]{2,1,0:T(8,128)(2,1)S(1)}, u32[]{:S(2)}, u32[]{:S(2)}) collective-permute-start(bf16[32,8,128]{2,1,0:T(8,128)(2,1)S(1)} %slice_bitcast_fusion.1), channel_id=1, source_target_pairs={{0,0},{8,1},{16,2},{24,3},{32,4},{40,5},{48,6},{56,7},{64,8},{72,9... | collective-permute-start | bytes 196616 | tf_op jit(solution)/shard_map/ppermute | solution.py:568
  143.3 13.0 %all-to-all-start.5 = ((bf16[8,2,128,128]{3,2,1,0:T(8,128)(2,1)}), bf16[8,2,128,128]{3,2,1,0:T(8,128)(2,1)S(1)}, u32[]{:S(2)}, u32[]{:S(2)}) async-start(bf16[8,2,128,128]{3,2,1,0:T(8,128)(2,1)} %broadcast_in_dim.33), calls=%async_computation.5 | async-start | bytes 1048576 | tf_op jit(solution)/shard_map/all_to_all | solution.py:491
  156.4 5.8 %collective-permute-start.4 = (bf16[9,128,128]{2,1,0:T(8,128)(2,1)S(1)}, bf16[9,128,128]{2,1,0:T(8,128)(2,1)S(1)}, u32[]{:S(2)}, u32[]{:S(2)}) collective-permute-start(bf16[9,128,128]{2,1,0:T(8,128)(2,1)S(1)} %pad_maximum_fusion.own_ref), channel_id=1, source_target_pairs={{0,8},{8,0},{16,24},{24,16},{32,40},{40,32},{48,56},{56,48},{64,72... | collective-permute-start | bytes 884744 | tf_op jit(solution)/shard_map/ppermute | solution.py:500

commit v4 on v3

--- a/solution.py
+++ b/solution.py
@@ -67,13 +67,12 @@
     rows = block * channels
     blocks = left_ref.shape[0] // rows
     chunk = 2 * lanes
-    early = rows - 2 * channels
-
-    def left_rows(b, start, size):
-        return left_ref[pl.ds(pl.multiple_of(b * rows + start, 2 * channels), size), :]
-
-    def outer_product(b, start, stop, at):
-        outer_scr[start:stop, at] = matmul(left_rows(b, start, stop - start), right_scr[:, at]).astype(BF16)
+
+    def left_rows(b):
+        return left_ref[pl.ds(pl.multiple_of(b * rows, rows), rows), :]
+
+    def outer_product(b, at):
+        outer_scr[:, at] = matmul(left_rows(b), right_scr[:, at]).astype(BF16)
 
     def pieces(h):
         each = wide // (4 * chunk)
@@ -109,11 +108,11 @@
         g_contract_ref[...] = jnp.zeros_like(g_contract_ref)
         for h in range(4):
             for at in pieces(h):
-                outer_product(0, 0, early, at)
+                outer_product(0, at)
 
     before = jnp.maximum(step - 1, 0)
     after = jnp.minimum(step + 1, blocks - 1)
-    left_t_scr[...] = left_rows(before, 0, rows).T
+    left_t_scr[...] = left_rows(before).T
 
     gain = jnp.broadcast_to(gain_ref[...], (2 * lanes, width)).T
     offset = jnp.broadcast_to(offset_ref[...], (2 * lanes, width)).T
@@ -188,29 +187,30 @@
         g_contract_ref[at, :] += matmul_nt(hidden_scr[p, at, :], st["cot"])
         g_expand_ref[at, :] += matmul_nt(d_hidden_scr[p, at, :], st["normed"])
 
-    last = None
     count = block // 2
+    ahead, last = forward(0), None
     for p in range(count + 1):
-        now = forward(p) if p < count else None
+        now = ahead if p < count else None
         if last is not None:
             through(last)
         for h in range(4):
+            if p == 0:
+                backward(before, h)
+            if h == 0 and p + 1 < count:
+                ahead = forward(p + 1)
             if now is not None:
                 activate(now, h)
             if last is not None:
+                pass
                 weigh(last, h)
-            if p == 0:
-                for at in pieces(h):
-                    outer_product(step, early, rows, at)
-                backward(before, h)
             if p == count:
                 for at in pieces(h):
-                    outer_product(after, 0, early, at)
+                    outer_product(after, at)
         last = now
 
     @pl.when(step == pl.num_programs(0) - 1)
     def _():
-        left_t_scr[...] = left_rows(step, 0, rows).T
+        left_t_scr[...] = left_rows(step).T
         for h in range(4):
             backward(step, h)
         each = own_ref.shape[2]

time: 164 us -> 161 us (0.982)
  Pallas kernels: 56.5 us -> 53.2 us
    pallas_call x1, Pallas kernels: 50.6 us -> 47.2 us  [pair_stage(): pl.pallas_call(pair_kernel, grid=(rows // block,), in_specs=[pl.BlockSpec...]
where the time goes in v4:
time: 161 us; the launch traced here: 160 us
  Pallas kernels  53.2 us (33%)
  blocking collectives  49.4 us (31%)
  starting transfers between devices  31.6 us (20%)
  waiting for transfers between devices  16.5 us (10%)
  local copies, waits for them, and re-layouts  6.73 us (4%)
  other arithmetic  1.64 us (1%)
    all_to_all x3, blocking collectives, exchange(): return lax.all_to_all(x, axis, 0, 0, tiled=True, axis_index_groups=groups)  49.4 us
    pallas_call x1, Pallas kernels, pair_stage(): pl.pallas_call(pair_kernel, grid=(rows // block,), in_specs=[pl.BlockSpec...  47.2 us
    all_to_all x3, starting transfers between devices, exchange(): return lax.all_to_all(x, axis, 0, 0, tiled=True, axis_index_groups=groups)  13.8 us
    all_to_all x3, waiting for transfers between devices, exchange(): return lax.all_to_all(x, axis, 0, 0, tiled=True, axis_index_groups=groups)  11.3 us
    ppermute x3, starting transfers between devices, from_partner(): lax.ppermute(x, 'row', [(k, k ^ 1) for k in range(lax.axis_size('row'))])  7.1 us
    ppermute x1, starting transfers between devices, on_device(): right_moved = lax.ppermute(right_local, BOTH, there)  6.04 us
    ppermute x3, waiting for transfers between devices, from_partner(): lax.ppermute(x, 'row', [(k, k ^ 1) for k in range(lax.axis_size('row'))])  4.88 us
    ppermute x1, starting transfers between devices, on_device(): d_right = lax.ppermute(d_right, BOTH, back)  4.74 us
  transfers between devices with their start and end apart: 8, of which 6 were waited for; matrix products, arithmetic and copies ran while one was open for 3% of the time, Pallas kernels for 1%

profile of v4, /device:TPU:1, one launch (start us, length us, event | category | flops | bytes accessed | tf_op | source)
XLA Modules:
  0.0 159.9 jit_solution(1484772410301042206)
XLA Ops:
  0.6 2.9 %project.1 = (bf16[8,8,32,128]{3,2,1,0:T(8,128)(2,1)}, bf16[32,8,128]{2,1,0:T(8,128)(2,1)}, bf16[8,128,256]{2,1,0:T(8,128)(2,1)}) custom-call(bf16[128,8,256]{2,1,0:T(8,128)(2,1)} %x_ref.3, f32[1,256]{1,0:T(1,128)} %bitcast.33, bf16[32,256]{1,0:T(8,128)(2,1)} %bitcast.29, bf16[32,256]{1,0:T(8,128)(2,1)} %bitcast.31), custom_call_target="tpu_custom_call" | custom-call | tf_op jit(solution)/shard_map/project/pallas_call | solution.py:400
  3.5 6.2 %all-to-all-start = ((bf16[8,8,32,128]{3,2,1,0:T(8,128)(2,1)}), bf16[8,8,32,128]{3,2,1,0:T(8,128)(2,1)S(1)}, u32[]{:S(2)}, u32[]{:S(2)}) async-start(bf16[8,8,32,128]{3,2,1,0:T(8,128)(2,1)} %get-tuple-element.32), calls=%async_computation | async-start | bytes 1048576 | tf_op jit(solution)/shard_map/all_to_all | solution.py:491
  9.7 6.0 %collective-permute-start = (bf16[32,8,128]{2,1,0:T(8,128)(2,1)}, bf16[32,8,128]{2,1,0:T(8,128)(2,1)S(1)}, u32[]{:S(2)}, u32[]{:S(2)}) collective-permute-start(bf16[32,8,128]{2,1,0:T(8,128)(2,1)} %get-tuple-element.31), channel_id=1, source_target_pairs={{0,0},{1,8},{2,16},{3,24},{4,32},{5,40},{6,48},{7,56},{8,64},{9,72... | collective-permute-start | bytes 196616 | tf_op jit(solution)/shard_map/ppermute | solution.py:540
  15.8 1.7 %copy.32 = bf16[128,512]{0,1:T(8,128)(2,1)} copy(bf16[128,512]{1,0:T(8,128)(2,1)} %expand_ref.1) | data formatting | bytes 262144 | tf_op args[8]
  17.4 1.7 %copy.33 = bf16[512,128]{0,1:T(8,128)(2,1)} copy(bf16[512,128]{1,0:T(8,128)(2,1)} %contract_ref.1) | data formatting | bytes 262144 | tf_op args[9]
  19.2 0.9 copy.31
  20.4 18.5 %all_to_all.30.own_ref = bf16[8,32,8,128]{3,2,1,0:T(8,128)(2,1)S(1)} all-to-all(bf16[8,32,8,128]{3,2,1,0:T(8,128)(2,1)S(1)} %broadcast_in_dim.30), channel_id=1, replica_groups={{0,16,32,48,64,80,96,112},{8,24,40,56,72,88,104,120},{1,17,33,49,65,81,..., dimensions={0} | all-to-all | bytes 1048576 | tf_op jit(solution)/shard_map/all_to_all | solution.py:491
  39.0 2.1 %collective-permute-start.1 = (bf16[8,32,8,128]{3,2,1,0:T(8,128)(2,1)S(1)}, bf16[8,32,8,128]{3,2,1,0:T(8,128)(2,1)S(1)}, u32[]{:S(2)}, u32[]{:S(2)}) collective-permute-start(bf16[8,32,8,128]{3,2,1,0:T(8,128)(2,1)S(1)} %all_to_all.30.own_ref), channel_id=1, source_target_pairs={{0,8},{8,0},{16,24},{24,16},{32,40},{40,32},{48,56},{56,48},{64,72... | collective-permute-start | bytes 1572872 | tf_op jit(solution)/shard_map/ppermute | solution.py:500
  41.1 1.5 collective-permute-done.1.other_ref
  43.4 47.2 %pair_stage.1 = (bf16[64,128,128]{2,1,0:T(8,128)(2,1)}, bf16[64,128,128]{2,1,0:T(8,128)(2,1)}, bf16[8,272,128]{2,1,0:T(8,128)(2,1)}, bf16[8,384,128]{2,1,0:T(8,128)(2,1)}, bf16[8,384,128]{2,1,0:T(8,128)(2,1)}) custom-call(s32[1]{0:T(128)} %bitcast.core_ref, bf16[2048,128]{1,0:T(8,128)(2,1)} %bitcast.37, bf16[8,32,8,128]{3,2,1,0:T(8,128)(2,1)} %copy-done.7, ...), custom_call_target="tpu_custom_call" | custom-call | tf_op jit(solution)/shard_map/pair_stage/pallas_call | solution.py:264
  91.1 2.1 %collective-permute-done.2 = bf16[8,384,128]{2,1,0:T(8,128)(2,1)S(1)} collective-permute-done((bf16[8,384,128]{2,1,0:T(8,128)(2,1)}, bf16[8,384,128]{2,1,0:T(8,128)(2,1)S(1)}, u32[]{:S(2)}, u32[]{:S(2)}) %collective-permute-start.2) | collective-permute-done | bytes 786464 | tf_op jit(solution)/shard_map/ppermute | solution.py:500
  93.2 1.3 add_convert_fusion
  94.6 17.1 %all_to_all.31 = bf16[8,384,128]{2,1,0:T(8,128)(2,1)S(1)} all-to-all(bf16[8,384,128]{2,1,0:T(8,128)(2,1)S(1)} %add_convert_fusion), channel_id=1, replica_groups={{0,16,32,48,64,80,96,112},{8,24,40,56,72,88,104,120},{1,17,33,49,65,81,..., dimensions={0} | all-to-all | bytes 1572864 | tf_op jit(solution)/shard_map/all_to_all | solution.py:491
  112.4 3.6 %all-to-all-start.3 = ((bf16[8,272,128]{2,1,0:T(8,128)(2,1)}), bf16[8,272,128]{2,1,0:T(8,128)(2,1)S(1)}, u32[]{:S(2)}, u32[]{:S(2)}) async-start(bf16[8,272,128]{2,1,0:T(8,128)(2,1)} %constant_dynamic-update-slice_fusion), calls=%async_computation.3 | async-start | bytes 1114112 | tf_op jit(solution)/shard_map/all_to_all | solution.py:491
  116.1 4.7 %collective-permute-start.3 = (bf16[32,8,128]{2,1,0:T(8,128)(2,1)S(1)}, bf16[32,8,128]{2,1,0:T(8,128)(2,1)S(1)}, u32[]{:S(2)}, u32[]{:S(2)}) collective-permute-start(bf16[32,8,128]{2,1,0:T(8,128)(2,1)S(1)} %slice_bitcast_fusion.1), channel_id=1, source_target_pairs={{0,0},{8,1},{16,2},{24,3},{32,4},{40,5},{48,6},{56,7},{64,8},{72,9... | collective-permute-start | bytes 196616 | tf_op jit(solution)/shard_map/ppermute | solution.py:568
  120.8 4.1 %all-to-all-done.3 = bf16[8,272,128]{2,1,0:T(8,128)(2,1)S(1)} async-done(((bf16[8,272,128]{2,1,0:T(8,128)(2,1)}), bf16[8,272,128]{2,1,0:T(8,128)(2,1)S(1)}, u32[]{:S(2)}, u32[]{:S(2)}) %all-to-all-start.3) | async-done | bytes 557088 | tf_op jit(solution)/shard_map/all_to_all | solution.py:491
  125.3 13.7 %all_to_all.32 = bf16[8,144,128]{2,1,0:T(8,128)(2,1)S(1)} all-to-all(bf16[8,144,128]{2,1,0:T(8,128)(2,1)S(1)} %factor_grad.1), channel_id=1, replica_groups=mesh['row'=16,'col'=8] {'col'}, dimensions={0} | all-to-all | bytes 589824 | tf_op jit(solution)/shard_map/all_to_all | solution.py:491
  139.1 0.9 broadcast_in_dim.33
  140.0 4.0 %all-to-all-start.5 = ((bf16[8,2,128,128]{3,2,1,0:T(8,128)(2,1)}), bf16[8,2,128,128]{3,2,1,0:T(8,128)(2,1)S(1)}, u32[]{:S(2)}, u32[]{:S(2)}) async-start(bf16[8,2,128,128]{3,2,1,0:T(8,128)(2,1)} %broadcast_in_dim.33), calls=%async_computation.5 | async-start | bytes 1048576 | tf_op jit(solution)/shard_map/all_to_all | solution.py:491
  144.0 1.8 %align_grad.1 = bf16[128,8,256]{2,1,0:T(8,128)(2,1)} custom-call(bf16[128,8,256]{2,1,0:T(8,128)(2,1)S(1)} %copy-done, f32[1,256]{1,0:T(1,128)S(1)} %bitcast.34, bf16[32,256]{1,0:T(8,128)(2,1)S(1)} %bitcast.30, bf16[32,256]{1,0:T(8,128)(2,1)S(1)} %bitcast.32, bf16[8,32,128]{2,1,0:T(8,128)(2,1)S(1)} %bitcast.28, ...), custom_call_target="tpu_custom_call" | custom-call | flops 78643200 | bytes 1310720 | tf_op jit(solution)/shard_map/align_grad/pallas_call | solution.py:470
  145.8 7.2 %all-to-all-done.5 = bf16[8,2,128,128]{3,2,1,0:T(8,128)(2,1)S(1)} async-done(((bf16[8,2,128,128]{3,2,1,0:T(8,128)(2,1)}), bf16[8,2,128,128]{3,2,1,0:T(8,128)(2,1)S(1)}, u32[]{:S(2)}, u32[]{:S(2)}) %all-to-all-start.5) | async-done | bytes 524320 | tf_op jit(solution)/shard_map/all_to_all | solution.py:491
  153.1 4.6 %collective-permute-start.4 = (bf16[9,128,128]{2,1,0:T(8,128)(2,1)S(1)}, bf16[9,128,128]{2,1,0:T(8,128)(2,1)S(1)}, u32[]{:S(2)}, u32[]{:S(2)}) collective-permute-start(bf16[9,128,128]{2,1,0:T(8,128)(2,1)S(1)} %pad_maximum_fusion.own_ref), channel_id=1, source_target_pairs={{0,8},{8,0},{16,24},{24,16},{32,40},{40,32},{48,56},{56,48},{64,72... | collective-permute-start | bytes 884744 | tf_op jit(solution)/shard_map/ppermute | solution.py:500
  157.6 1.2 collective-permute-done.4.other_ref
  158.9 1.0 unpack.1
  (39 shorter events, 3.0 us)
Async XLA Ops:
  0.6 18.5 %copy-start.9 = (bf16[1024,128]{1,0:T(8,128)(2,1)S(1)}, bf16[1024,128]{1,0:T(8,128)(2,1)}, u32[]{:S(2)}) copy-start(bf16[1024,128]{1,0:T(8,128)(2,1)} %param.15) | copy-start | bytes 786436
  3.5 16.8 %all-to-all-start = ((bf16[8,8,32,128]{3,2,1,0:T(8,128)(2,1)}), bf16[8,8,32,128]{3,2,1,0:T(8,128)(2,1)S(1)}, u32[]{:S(2)}, u32[]{:S(2)}) async-start(bf16[8,8,32,128]{3,2,1,0:T(8,128)(2,1)} %get-tuple-element.32), calls=%async_computation | async-start | bytes 1048576 | tf_op jit(solution)/shard_map/all_to_all | solution.py:491
  9.7 10.6 %collective-permute-start = (bf16[32,8,128]{2,1,0:T(8,128)(2,1)}, bf16[32,8,128]{2,1,0:T(8,128)(2,1)S(1)}, u32[]{:S(2)}, u32[]{:S(2)}) collective-permute-start(bf16[32,8,128]{2,1,0:T(8,128)(2,1)} %get-tuple-element.31), channel_id=1, source_target_pairs={{0,0},{1,8},{2,16},{3,24},{4,32},{5,40},{6,48},{7,56},{8,64},{9,72... | collective-permute-start | bytes 196616 | tf_op jit(solution)/shard_map/ppermute | solution.py:540
  19.2 23.4 %copy-start.5 = (bf16[32,32,128]{2,1,0:T(8,128)(2,1)}, bf16[32,32,128]{2,1,0:T(8,128)(2,1)S(1)}, u32[]{:S(2)}) copy-start(bf16[32,32,128]{2,1,0:T(8,128)(2,1)S(1)} %copy.30) | copy-start | bytes 786436
  20.4 22.3 %copy-start.6 = (bf16[8,8,32,128]{3,2,1,0:T(8,128)(2,1)}, bf16[8,8,32,128]{3,2,1,0:T(8,128)(2,1)S(1)}, u32[]{:S(2)}) copy-start(bf16[8,8,32,128]{3,2,1,0:T(8,128)(2,1)S(1)} %all-to-all-done) | copy-start | bytes 1572868
  39.0 3.6 %copy-start.7 = (bf16[8,32,8,128]{3,2,1,0:T(8,128)(2,1)}, bf16[8,32,8,128]{3,2,1,0:T(8,128)(2,1)S(1)}, u32[]{:S(2)}) copy-start(bf16[8,32,8,128]{3,2,1,0:T(8,128)(2,1)S(1)} %all_to_all.30.own_ref) | copy-start | bytes 1572868
  39.0 3.6 %collective-permute-start.1 = (bf16[8,32,8,128]{3,2,1,0:T(8,128)(2,1)S(1)}, bf16[8,32,8,128]{3,2,1,0:T(8,128)(2,1)S(1)}, u32[]{:S(2)}, u32[]{:S(2)}) collective-permute-start(bf16[8,32,8,128]{3,2,1,0:T(8,128)(2,1)S(1)} %all_to_all.30.own_ref), channel_id=1, source_target_pairs={{0,8},{8,0},{16,24},{24,16},{32,40},{40,32},{48,56},{56,48},{64,72... | collective-permute-start | bytes 1572872 | tf_op jit(solution)/shard_map/ppermute | solution.py:500
  42.6 0.8 copy-start.8
  90.7 2.6 %collective-permute-start.2 = (bf16[8,384,128]{2,1,0:T(8,128)(2,1)}, bf16[8,384,128]{2,1,0:T(8,128)(2,1)S(1)}, u32[]{:S(2)}, u32[]{:S(2)}) collective-permute-start(bf16[8,384,128]{2,1,0:T(8,128)(2,1)} %get-tuple-element.43), channel_id=1, source_target_pairs={{0,8},{8,0},{16,24},{24,16},{32,40},{40,32},{48,56},{56,48},{64,72... | collective-permute-start | bytes 2359304 | tf_op jit(solution)/shard_map/ppermute | solution.py:500
  94.6 30.4 %copy-start.1 = (bf16[8,128,256]{2,1,0:T(8,128)(2,1)S(1)}, bf16[8,128,256]{2,1,0:T(8,128)(2,1)}, u32[]{:S(2)}) copy-start(bf16[8,128,256]{2,1,0:T(8,128)(2,1)} %get-tuple-element.41.normed_ref) | copy-start | bytes 1572868
  112.4 12.5 %all-to-all-start.3 = ((bf16[8,272,128]{2,1,0:T(8,128)(2,1)}), bf16[8,272,128]{2,1,0:T(8,128)(2,1)S(1)}, u32[]{:S(2)}, u32[]{:S(2)}) async-start(bf16[8,272,128]{2,1,0:T(8,128)(2,1)} %constant_dynamic-update-slice_fusion), calls=%async_computation.3 | async-start | bytes 1114112 | tf_op jit(solution)/shard_map/all_to_all | solution.py:491
  116.0 27.9 %copy-start = (bf16[128,8,256]{2,1,0:T(8,128)(2,1)S(1)}, bf16[128,8,256]{2,1,0:T(8,128)(2,1)}, u32[]{:S(2)}) copy-start(bf16[128,8,256]{2,1,0:T(8,128)(2,1)} %x_ref.3) | copy-start | bytes 1572868
  116.0 27.9 %copy-start.2 = (bf16[256,32]{0,1:T(8,128)(2,1)S(1)}, bf16[256,32]{0,1:T(8,128)(2,1)}, u32[]{:S(2)}) copy-start(bf16[256,32]{0,1:T(8,128)(2,1)} %param.13) | copy-start | bytes 49156
  116.1 27.9 %copy-start.3 = (bf16[256,32]{0,1:T(8,128)(2,1)S(1)}, bf16[256,32]{0,1:T(8,128)(2,1)}, u32[]{:S(2)}) copy-start(bf16[256,32]{0,1:T(8,128)(2,1)} %param.14) | copy-start | bytes 49156
  116.1 27.9 %copy-start.4 = (f32[256]{0:T(256)S(1)}, f32[256]{0:T(256)}, u32[]{:S(2)}) copy-start(f32[256]{0:T(256)} %param.12) | copy-start | bytes 3076
  116.1 8.9 %collective-permute-start.3 = (bf16[32,8,128]{2,1,0:T(8,128)(2,1)S(1)}, bf16[32,8,128]{2,1,0:T(8,128)(2,1)S(1)}, u32[]{:S(2)}, u32[]{:S(2)}) collective-permute-start(bf16[32,8,128]{2,1,0:T(8,128)(2,1)S(1)} %slice_bitcast_fusion.1), channel_id=1, source_target_pairs={{0,0},{8,1},{16,2},{24,3},{32,4},{40,5},{48,6},{56,7},{64,8},{72,9... | collective-permute-start | bytes 196616 | tf_op jit(solution)/shard_map/ppermute | solution.py:568
  140.0 13.0 %all-to-all-start.5 = ((bf16[8,2,128,128]{3,2,1,0:T(8,128)(2,1)}), bf16[8,2,128,128]{3,2,1,0:T(8,128)(2,1)S(1)}, u32[]{:S(2)}, u32[]{:S(2)}) async-start(bf16[8,2,128,128]{3,2,1,0:T(8,128)(2,1)} %broadcast_in_dim.33), calls=%async_computation.5 | async-start | bytes 1048576 | tf_op jit(solution)/shard_map/all_to_all | solution.py:491
  153.1 5.8 %collective-permute-start.4 = (bf16[9,128,128]{2,1,0:T(8,128)(2,1)S(1)}, bf16[9,128,128]{2,1,0:T(8,128)(2,1)S(1)}, u32[]{:S(2)}, u32[]{:S(2)}) collective-permute-start(bf16[9,128,128]{2,1,0:T(8,128)(2,1)S(1)} %pad_maximum_fusion.own_ref), channel_id=1, source_target_pairs={{0,8},{8,0},{16,24},{24,16},{32,40},{40,32},{48,56},{56,48},{64,72... | collective-permute-start | bytes 884744 | tf_op jit(solution)/shard_map/ppermute | solution.py:500

commit v5 on v4

--- a/solution.py
+++ b/solution.py
@@ -194,10 +194,10 @@
         if last is not None:
             through(last)
         for h in range(4):
+            if h == 0 and p + 1 < count:
+                ahead = forward(p + 1)
             if p == 0:
                 backward(before, h)
-            if h == 0 and p + 1 < count:
-                ahead = forward(p + 1)
             if now is not None:
                 activate(now, h)
             if last is not None:
@@ -438,6 +438,27 @@
     )(normed, left, right, weights)
 
 
+def regroup_kernel(parts_ref, out_ref):
+    count = out_ref.shape[2]
+    factors = jnp.sum(parts_ref[:, :count, :].astype(F32), axis=0).astype(BF16)
+    weights = parts_ref[:, count:, :].reshape(out_ref.shape[2:])
+    for k in range(out_ref.shape[0]):
+        out_ref[k, 0] = factors
+        out_ref[k, 1] = weights
+
+
+def regroup(parts, count, copies):
+    vmem = pl.BlockSpec(memory_space=pltpu.VMEM)
+    return pl.pallas_call(
+        regroup_kernel,
+        in_specs=[vmem],
+        out_specs=vmem,
+        out_shape=jax.ShapeDtypeStruct((copies, 2, count, parts.shape[2]), BF16),
+        compiler_params=pltpu.CompilerParams(vmem_limit_bytes=16 * 1024 * 1024),
+        name="regroup",
+    )(parts)
+
+
 def align_grad_kernel(x_ref, gain_ref, first_ref, second_ref, left_ref, right_ref, out_ref, *halves):
     seqs, residues, features = x_ref.shape
     lanes = halves[0].shape[1]
@@ -572,9 +593,7 @@
 
     gathered = exchange(factor_grad(normed, d_left, d_right, weights, cols), "col")
     count = gathered.shape[1] - weights.shape[0]
-    factors = summed(gathered[:, :count])
-    weights = gathered[:, count:].reshape(-1, lanes)
-    gathered = spread(jnp.stack([factors, weights], axis=0), "row")
+    gathered = exchange(regroup(gathered, count, rows // 2), "row")
     alignment_sensitivity = align_grad(
         alignment_tensor, gain, first_t, second_t, d_left, d_right
     )

time: 161 us -> 160 us (level)
  no operation moved by 1% of the time
where the time goes in v5:
time: 160 us; the launch traced here: 159 us
  Pallas kernels  53.7 us (34%)
  blocking collectives  49.4 us (31%)
  starting transfers between devices  31.6 us (20%)
  waiting for transfers between devices  16.4 us (10%)
  local copies, waits for them, and re-layouts  5.84 us (4%)
  other arithmetic  1.6 us (1%)
    all_to_all x3, blocking collectives, exchange(): return lax.all_to_all(x, axis, 0, 0, tiled=True, axis_index_groups=groups)  49.4 us
    pallas_call x1, Pallas kernels, pair_stage(): pl.pallas_call(pair_kernel, grid=(rows // block,), in_specs=[pl.BlockSpec...  46.9 us
    all_to_all x3, starting transfers between devices, exchange(): return lax.all_to_all(x, axis, 0, 0, tiled=True, axis_index_groups=groups)  13.8 us
    all_to_all x3, waiting for transfers between devices, exchange(): return lax.all_to_all(x, axis, 0, 0, tiled=True, axis_index_groups=groups)  11.3 us
    ppermute x3, starting transfers between devices, from_partner(): lax.ppermute(x, 'row', [(k, k ^ 1) for k in range(lax.axis_size('row'))])  7.12 us
    ppermute x1, starting transfers between devices, on_device(): right_moved = lax.ppermute(right_local, BOTH, there)  6.04 us
    ppermute x3, waiting for transfers between devices, from_partner(): lax.ppermute(x, 'row', [(k, k ^ 1) for k in range(lax.axis_size('row'))])  4.87 us
    ppermute x1, starting transfers between devices, on_device(): d_right = lax.ppermute(d_right, BOTH, back)  4.74 us
  transfers between devices with their start and end apart: 8, of which 6 were waited for; matrix products, arithmetic and copies ran while one was open for 3% of the time, Pallas kernels for 1%

profile of v5, /device:TPU:1, one launch (start us, length us, event | category | flops | bytes accessed | tf_op | source)
XLA Modules:
  0.0 159.4 jit_solution(9219427474039277475)
XLA Ops:
  0.6 2.9 %project.1 = (bf16[8,8,32,128]{3,2,1,0:T(8,128)(2,1)}, bf16[32,8,128]{2,1,0:T(8,128)(2,1)}, bf16[8,128,256]{2,1,0:T(8,128)(2,1)}) custom-call(bf16[128,8,256]{2,1,0:T(8,128)(2,1)} %x_ref.3, f32[1,256]{1,0:T(1,128)} %bitcast.31, bf16[32,256]{1,0:T(8,128)(2,1)} %bitcast.27, bf16[32,256]{1,0:T(8,128)(2,1)} %bitcast.29), custom_call_target="tpu_custom_call" | custom-call | tf_op jit(solution)/shard_map/project/pallas_call | solution.py:400
  3.5 6.2 %all-to-all-start = ((bf16[8,8,32,128]{3,2,1,0:T(8,128)(2,1)}), bf16[8,8,32,128]{3,2,1,0:T(8,128)(2,1)S(1)}, u32[]{:S(2)}, u32[]{:S(2)}) async-start(bf16[8,8,32,128]{3,2,1,0:T(8,128)(2,1)} %get-tuple-element.32), calls=%async_computation | async-start | bytes 1048576 | tf_op jit(solution)/shard_map/all_to_all | solution.py:512
  9.7 6.0 %collective-permute-start = (bf16[32,8,128]{2,1,0:T(8,128)(2,1)}, bf16[32,8,128]{2,1,0:T(8,128)(2,1)S(1)}, u32[]{:S(2)}, u32[]{:S(2)}) collective-permute-start(bf16[32,8,128]{2,1,0:T(8,128)(2,1)} %get-tuple-element.31), channel_id=1, source_target_pairs={{0,0},{1,8},{2,16},{3,24},{4,32},{5,40},{6,48},{7,56},{8,64},{9,72... | collective-permute-start | bytes 196616 | tf_op jit(solution)/shard_map/ppermute | solution.py:561
  15.8 1.7 %copy.35 = bf16[128,512]{0,1:T(8,128)(2,1)} copy(bf16[128,512]{1,0:T(8,128)(2,1)} %expand_ref.1) | data formatting | bytes 262144 | tf_op args[8]
  17.5 1.7 %copy.36 = bf16[512,128]{0,1:T(8,128)(2,1)} copy(bf16[512,128]{1,0:T(8,128)(2,1)} %contract_ref.1) | data formatting | bytes 262144 | tf_op args[9]
  19.2 0.9 copy.34
  20.4 18.5 %all_to_all.30.own_ref = bf16[8,32,8,128]{3,2,1,0:T(8,128)(2,1)S(1)} all-to-all(bf16[8,32,8,128]{3,2,1,0:T(8,128)(2,1)S(1)} %broadcast_in_dim.24), channel_id=1, replica_groups={{0,16,32,48,64,80,96,112},{8,24,40,56,72,88,104,120},{1,17,33,49,65,81,..., dimensions={0} | all-to-all | bytes 1048576 | tf_op jit(solution)/shard_map/all_to_all | solution.py:512
  39.0 2.1 %collective-permute-start.1 = (bf16[8,32,8,128]{3,2,1,0:T(8,128)(2,1)S(1)}, bf16[8,32,8,128]{3,2,1,0:T(8,128)(2,1)S(1)}, u32[]{:S(2)}, u32[]{:S(2)}) collective-permute-start(bf16[8,32,8,128]{3,2,1,0:T(8,128)(2,1)S(1)} %all_to_all.30.own_ref), channel_id=1, source_target_pairs={{0,8},{8,0},{16,24},{24,16},{32,40},{40,32},{48,56},{56,48},{64,72... | collective-permute-start | bytes 1572872 | tf_op jit(solution)/shard_map/ppermute | solution.py:521
  41.1 1.5 collective-permute-done.1.other_ref
  43.4 46.9 %pair_stage.1 = (bf16[64,128,128]{2,1,0:T(8,128)(2,1)}, bf16[64,128,128]{2,1,0:T(8,128)(2,1)}, bf16[8,272,128]{2,1,0:T(8,128)(2,1)}, bf16[8,384,128]{2,1,0:T(8,128)(2,1)}, bf16[8,384,128]{2,1,0:T(8,128)(2,1)}) custom-call(s32[1]{0:T(128)} %bitcast.core_ref, bf16[2048,128]{1,0:T(8,128)(2,1)} %bitcast.35, bf16[8,32,8,128]{3,2,1,0:T(8,128)(2,1)} %copy-done.7, ...), custom_call_target="tpu_custom_call" | custom-call | tf_op jit(solution)/shard_map/pair_stage/pallas_call | solution.py:264
  90.8 2.1 %collective-permute-done.2 = bf16[8,384,128]{2,1,0:T(8,128)(2,1)S(1)} collective-permute-done((bf16[8,384,128]{2,1,0:T(8,128)(2,1)}, bf16[8,384,128]{2,1,0:T(8,128)(2,1)S(1)}, u32[]{:S(2)}, u32[]{:S(2)}) %collective-permute-start.2) | collective-permute-done | bytes 786464 | tf_op jit(solution)/shard_map/ppermute | solution.py:521
  92.9 1.3 add_convert_fusion
  94.3 17.1 %all_to_all.31 = bf16[8,384,128]{2,1,0:T(8,128)(2,1)S(1)} all-to-all(bf16[8,384,128]{2,1,0:T(8,128)(2,1)S(1)} %add_convert_fusion), channel_id=1, replica_groups={{0,16,32,48,64,80,96,112},{8,24,40,56,72,88,104,120},{1,17,33,49,65,81,..., dimensions={0} | all-to-all | bytes 1572864 | tf_op jit(solution)/shard_map/all_to_all | solution.py:512
  112.1 3.6 %all-to-all-start.3 = ((bf16[8,272,128]{2,1,0:T(8,128)(2,1)}), bf16[8,272,128]{2,1,0:T(8,128)(2,1)S(1)}, u32[]{:S(2)}, u32[]{:S(2)}) async-start(bf16[8,272,128]{2,1,0:T(8,128)(2,1)} %constant_dynamic-update-slice_fusion), calls=%async_computation.3 | async-start | bytes 1114112 | tf_op jit(solution)/shard_map/all_to_all | solution.py:512
  115.8 4.7 %collective-permute-start.3 = (bf16[32,8,128]{2,1,0:T(8,128)(2,1)S(1)}, bf16[32,8,128]{2,1,0:T(8,128)(2,1)S(1)}, u32[]{:S(2)}, u32[]{:S(2)}) collective-permute-start(bf16[32,8,128]{2,1,0:T(8,128)(2,1)S(1)} %slice_bitcast_fusion.1), channel_id=1, source_target_pairs={{0,0},{8,1},{16,2},{24,3},{32,4},{40,5},{48,6},{56,7},{64,8},{72,9... | collective-permute-start | bytes 196616 | tf_op jit(solution)/shard_map/ppermute | solution.py:589
  120.5 4.1 %all-to-all-done.3 = bf16[8,272,128]{2,1,0:T(8,128)(2,1)S(1)} async-done(((bf16[8,272,128]{2,1,0:T(8,128)(2,1)}), bf16[8,272,128]{2,1,0:T(8,128)(2,1)S(1)}, u32[]{:S(2)}, u32[]{:S(2)}) %all-to-all-start.3) | async-done | bytes 557088 | tf_op jit(solution)/shard_map/all_to_all | solution.py:512
  125.0 13.7 %all_to_all.32.parts_ref = bf16[8,144,128]{2,1,0:T(8,128)(2,1)S(1)} all-to-all(bf16[8,144,128]{2,1,0:T(8,128)(2,1)S(1)} %factor_grad.1), channel_id=1, replica_groups=mesh['row'=16,'col'=8] {'col'}, dimensions={0} | all-to-all | bytes 589824 | tf_op jit(solution)/shard_map/all_to_all | solution.py:512
  138.7 0.9 regroup.1
  139.6 4.0 %all-to-all-start.5 = ((bf16[8,2,128,128]{3,2,1,0:T(8,128)(2,1)}), bf16[8,2,128,128]{3,2,1,0:T(8,128)(2,1)S(1)}, u32[]{:S(2)}, u32[]{:S(2)}) async-start(bf16[8,2,128,128]{3,2,1,0:T(8,128)(2,1)} %regroup.1), calls=%async_computation.5 | async-start | bytes 1048576 | tf_op jit(solution)/shard_map/all_to_all | solution.py:512
  143.6 1.8 %align_grad.1 = bf16[128,8,256]{2,1,0:T(8,128)(2,1)} custom-call(bf16[128,8,256]{2,1,0:T(8,128)(2,1)S(1)} %copy-done, f32[1,256]{1,0:T(1,128)S(1)} %bitcast.32, bf16[32,256]{1,0:T(8,128)(2,1)S(1)} %bitcast.28, bf16[32,256]{1,0:T(8,128)(2,1)S(1)} %bitcast.30, bf16[8,32,128]{2,1,0:T(8,128)(2,1)S(1)} %bitcast.26, ...), custom_call_target="tpu_custom_call" | custom-call | flops 78643200 | bytes 1310720 | tf_op jit(solution)/shard_map/align_grad/pallas_call | solution.py:491
  145.3 7.2 %all-to-all-done.5 = bf16[8,2,128,128]{3,2,1,0:T(8,128)(2,1)S(1)} async-done(((bf16[8,2,128,128]{3,2,1,0:T(8,128)(2,1)}), bf16[8,2,128,128]{3,2,1,0:T(8,128)(2,1)S(1)}, u32[]{:S(2)}, u32[]{:S(2)}) %all-to-all-start.5) | async-done | bytes 524320 | tf_op jit(solution)/shard_map/all_to_all | solution.py:512
  152.7 4.6 %collective-permute-start.4 = (bf16[9,128,128]{2,1,0:T(8,128)(2,1)S(1)}, bf16[9,128,128]{2,1,0:T(8,128)(2,1)S(1)}, u32[]{:S(2)}, u32[]{:S(2)}) collective-permute-start(bf16[9,128,128]{2,1,0:T(8,128)(2,1)S(1)} %pad_maximum_fusion.own_ref), channel_id=1, source_target_pairs={{0,8},{8,0},{16,24},{24,16},{32,40},{40,32},{48,56},{56,48},{64,72... | collective-permute-start | bytes 884744 | tf_op jit(solution)/shard_map/ppermute | solution.py:521
  157.2 1.2 collective-permute-done.4.other_ref
  158.4 1.0 unpack.1
  (36 shorter events, 2.9 us)
Async XLA Ops:
  0.6 18.5 %copy-start.9 = (bf16[1024,128]{1,0:T(8,128)(2,1)S(1)}, bf16[1024,128]{1,0:T(8,128)(2,1)}, u32[]{:S(2)}) copy-start(bf16[1024,128]{1,0:T(8,128)(2,1)} %param.15) | copy-start | bytes 786436
  3.5 16.8 %all-to-all-start = ((bf16[8,8,32,128]{3,2,1,0:T(8,128)(2,1)}), bf16[8,8,32,128]{3,2,1,0:T(8,128)(2,1)S(1)}, u32[]{:S(2)}, u32[]{:S(2)}) async-start(bf16[8,8,32,128]{3,2,1,0:T(8,128)(2,1)} %get-tuple-element.32), calls=%async_computation | async-start | bytes 1048576 | tf_op jit(solution)/shard_map/all_to_all | solution.py:512
  9.7 10.6 %collective-permute-start = (bf16[32,8,128]{2,1,0:T(8,128)(2,1)}, bf16[32,8,128]{2,1,0:T(8,128)(2,1)S(1)}, u32[]{:S(2)}, u32[]{:S(2)}) collective-permute-start(bf16[32,8,128]{2,1,0:T(8,128)(2,1)} %get-tuple-element.31), channel_id=1, source_target_pairs={{0,0},{1,8},{2,16},{3,24},{4,32},{5,40},{6,48},{7,56},{8,64},{9,72... | collective-permute-start | bytes 196616 | tf_op jit(solution)/shard_map/ppermute | solution.py:561
  19.2 23.4 %copy-start.5 = (bf16[32,32,128]{2,1,0:T(8,128)(2,1)}, bf16[32,32,128]{2,1,0:T(8,128)(2,1)S(1)}, u32[]{:S(2)}) copy-start(bf16[32,32,128]{2,1,0:T(8,128)(2,1)S(1)} %copy.33) | copy-start | bytes 786436
  20.4 22.3 %copy-start.6 = (bf16[8,8,32,128]{3,2,1,0:T(8,128)(2,1)}, bf16[8,8,32,128]{3,2,1,0:T(8,128)(2,1)S(1)}, u32[]{:S(2)}) copy-start(bf16[8,8,32,128]{3,2,1,0:T(8,128)(2,1)S(1)} %all-to-all-done) | copy-start | bytes 1572868
  39.0 3.6 %copy-start.7 = (bf16[8,32,8,128]{3,2,1,0:T(8,128)(2,1)}, bf16[8,32,8,128]{3,2,1,0:T(8,128)(2,1)S(1)}, u32[]{:S(2)}) copy-start(bf16[8,32,8,128]{3,2,1,0:T(8,128)(2,1)S(1)} %all_to_all.30.own_ref) | copy-start | bytes 1572868
  39.0 3.6 %collective-permute-start.1 = (bf16[8,32,8,128]{3,2,1,0:T(8,128)(2,1)S(1)}, bf16[8,32,8,128]{3,2,1,0:T(8,128)(2,1)S(1)}, u32[]{:S(2)}, u32[]{:S(2)}) collective-permute-start(bf16[8,32,8,128]{3,2,1,0:T(8,128)(2,1)S(1)} %all_to_all.30.own_ref), channel_id=1, source_target_pairs={{0,8},{8,0},{16,24},{24,16},{32,40},{40,32},{48,56},{56,48},{64,72... | collective-permute-start | bytes 1572872 | tf_op jit(solution)/shard_map/ppermute | solution.py:521
  42.6 0.8 copy-start.8
  90.3 2.6 %collective-permute-start.2 = (bf16[8,384,128]{2,1,0:T(8,128)(2,1)}, bf16[8,384,128]{2,1,0:T(8,128)(2,1)S(1)}, u32[]{:S(2)}, u32[]{:S(2)}) collective-permute-start(bf16[8,384,128]{2,1,0:T(8,128)(2,1)} %get-tuple-element.43), channel_id=1, source_target_pairs={{0,8},{8,0},{16,24},{24,16},{32,40},{40,32},{48,56},{56,48},{64,72... | collective-permute-start | bytes 2359304 | tf_op jit(solution)/shard_map/ppermute | solution.py:521
  94.2 30.4 %copy-start.1 = (bf16[8,128,256]{2,1,0:T(8,128)(2,1)S(1)}, bf16[8,128,256]{2,1,0:T(8,128)(2,1)}, u32[]{:S(2)}) copy-start(bf16[8,128,256]{2,1,0:T(8,128)(2,1)} %get-tuple-element.41.normed_ref) | copy-start | bytes 1572868
  112.1 12.4 %all-to-all-start.3 = ((bf16[8,272,128]{2,1,0:T(8,128)(2,1)}), bf16[8,272,128]{2,1,0:T(8,128)(2,1)S(1)}, u32[]{:S(2)}, u32[]{:S(2)}) async-start(bf16[8,272,128]{2,1,0:T(8,128)(2,1)} %constant_dynamic-update-slice_fusion), calls=%async_computation.3 | async-start | bytes 1114112 | tf_op jit(solution)/shard_map/all_to_all | solution.py:512
  115.7 27.8 %copy-start = (bf16[128,8,256]{2,1,0:T(8,128)(2,1)S(1)}, bf16[128,8,256]{2,1,0:T(8,128)(2,1)}, u32[]{:S(2)}) copy-start(bf16[128,8,256]{2,1,0:T(8,128)(2,1)} %x_ref.3) | copy-start | bytes 1572868
  115.7 27.8 %copy-start.2 = (bf16[256,32]{0,1:T(8,128)(2,1)S(1)}, bf16[256,32]{0,1:T(8,128)(2,1)}, u32[]{:S(2)}) copy-start(bf16[256,32]{0,1:T(8,128)(2,1)} %param.13) | copy-start | bytes 49156
  115.7 27.8 %copy-start.3 = (bf16[256,32]{0,1:T(8,128)(2,1)S(1)}, bf16[256,32]{0,1:T(8,128)(2,1)}, u32[]{:S(2)}) copy-start(bf16[256,32]{0,1:T(8,128)(2,1)} %param.14) | copy-start | bytes 49156
  115.7 27.8 %copy-start.4 = (f32[256]{0:T(256)S(1)}, f32[256]{0:T(256)}, u32[]{:S(2)}) copy-start(f32[256]{0:T(256)} %param.12) | copy-start | bytes 3076
  115.8 8.9 %collective-permute-start.3 = (bf16[32,8,128]{2,1,0:T(8,128)(2,1)S(1)}, bf16[32,8,128]{2,1,0:T(8,128)(2,1)S(1)}, u32[]{:S(2)}, u32[]{:S(2)}) collective-permute-start(bf16[32,8,128]{2,1,0:T(8,128)(2,1)S(1)} %slice_bitcast_fusion.1), channel_id=1, source_target_pairs={{0,0},{8,1},{16,2},{24,3},{32,4},{40,5},{48,6},{56,7},{64,8},{72,9... | collective-permute-start | bytes 196616 | tf_op jit(solution)/shard_map/ppermute | solution.py:589
  139.6 13.0 %all-to-all-start.5 = ((bf16[8,2,128,128]{3,2,1,0:T(8,128)(2,1)}), bf16[8,2,128,128]{3,2,1,0:T(8,128)(2,1)S(1)}, u32[]{:S(2)}, u32[]{:S(2)}) async-start(bf16[8,2,128,128]{3,2,1,0:T(8,128)(2,1)} %regroup.1), calls=%async_computation.5 | async-start | bytes 1048576 | tf_op jit(solution)/shard_map/all_to_all | solution.py:512
  152.7 5.8 %collective-permute-start.4 = (bf16[9,128,128]{2,1,0:T(8,128)(2,1)S(1)}, bf16[9,128,128]{2,1,0:T(8,128)(2,1)S(1)}, u32[]{:S(2)}, u32[]{:S(2)}) collective-permute-start(bf16[9,128,128]{2,1,0:T(8,128)(2,1)S(1)} %pad_maximum_fusion.own_ref), channel_id=1, source_target_pairs={{0,8},{8,0},{16,24},{24,16},{32,40},{40,32},{48,56},{56,48},{64,72... | collective-permute-start | bytes 884744 | tf_op jit(solution)/shard_map/ppermute | solution.py:521
